TPU v7x, 32 devices: a whole 2x2x4 slice. The times are simulated.
32 devices in a mesh: tm: 1, space: 32 (over z, y, x, core).
Axes of the slice: x: 2, y: 2, z: 4, core: 2. Of those that a mesh axis runs over, the one named last changes fastest.
Arguments:
- links: float32 [8, 3, 2, 3, 2, 110592], P('tm', None, None, None, None, 'space'), may hold values from -1 to 1, as said below
Outputs:
- new_links: float32 [8, 3, 2, 3, 2, 110592], P('tm', None, None, None, None, 'space')
- theta: float32 [], replicated
- deficit: float32 [8], P('tm')
Inputs may be any that keep to these rules, and one draw needn't show every extreme that they name: `links`: each link's two stored rows are orthonormal complex 3-vectors, the first two rows of a special unitary matrix.
All inputs are finite; a program needn't handle non-finite values.
Results may differ from a plain program's by a relative error of at most 0.00013.
Values sent between devices are 32-bit elements; how exact they have to be, the bound alone decides.
A program may use at most 128 MiB of HBM per device.

v0:
```python
import math

import jax
import jax.numpy as jnp
from jax import lax
from jax.sharding import PartitionSpec as P

EXTENT = 48


root_three = math.sqrt(3.0)
step_size = 0.08
top_momentum = 12.0
storage_offset = 1


def from_behind(block, axis, distance):
    devices = range(lax.axis_size(axis))
    route = [((i - distance) % len(devices), i) for i in devices]
    return lax.ppermute(block, axis, route)


def complex_mul(p, q):
    return (p[0] * q[0] - p[1] * q[1], p[0] * q[1] + p[1] * q[0])


def complex_add(p, q):
    return (p[0] + q[0], p[1] + q[1])


def complex_sub(p, q):
    return (p[0] - q[0], p[1] - q[1])


def complex_conj(p):
    return (p[0], -p[1])


def matrix_mul(left, right):
    rows_out = []
    for i in range(len(left)):
        entries = []
        for j in range(3):
            summed = complex_mul(left[i][0], right[0][j])
            for k in (1, 2):
                summed = complex_add(summed, complex_mul(left[i][k], right[k][j]))
            entries.append(summed)
        rows_out.append(entries)
    return rows_out


def dagger_of(matrix):
    return [[complex_conj(matrix[j][i]) for j in range(3)] for i in range(3)]


def cross_conj(row_one, row_two):
    row_three = []
    for k in range(3):
        a = complex_mul(row_one[(k + 1) % 3], row_two[(k + 2) % 3])
        b = complex_mul(row_one[(k + 2) % 3], row_two[(k + 1) % 3])
        row_three.append(complex_conj(complex_sub(a, b)))
    return row_three


def full_matrix(entry_of):
    row_one = [(entry_of(0, c, 0), entry_of(0, c, 1)) for c in range(3)]
    row_two = [(entry_of(1, c, 0), entry_of(1, c, 1)) for c in range(3)]
    return [row_one, row_two, cross_conj(row_one, row_two)]


def link_matrix(arr):
    return full_matrix(lambda r, c, p: arr[:, r, c, p])


def gradient_of(current, behind):
    gradient = []
    for i in range(3):
        entries = []
        for j in range(3):
            summed = complex_sub(behind[0][i][j], current[0][i][j])
            for d in (1, 2):
                summed = complex_add(summed, complex_sub(behind[d][i][j], current[d][i][j]))
            entries.append(summed)
        gradient.append(entries)
    return gradient


def algebra_of(gradient):
    return [
        gradient[0][1][1] + gradient[1][0][1],
        gradient[0][1][0] - gradient[1][0][0],
        gradient[0][0][1] - gradient[1][1][1],
        gradient[0][2][1] + gradient[2][0][1],
        gradient[0][2][0] - gradient[2][0][0],
        gradient[1][2][1] + gradient[2][1][1],
        gradient[1][2][0] - gradient[2][1][0],
        (gradient[0][0][1] + gradient[1][1][1] - 2.0 * gradient[2][2][1]) / root_three,
    ]


def rotation_of(algebra):
    half_step = 0.5 * step_size
    zeros_like = jnp.zeros_like(algebra[0])
    diag_zero = algebra[2] + algebra[7] / root_three
    diag_one = -algebra[2] + algebra[7] / root_three
    diag_two = -2.0 * algebra[7] / root_three
    hermitian = [
        [(diag_zero, zeros_like), (algebra[0], -algebra[1]), (algebra[3], -algebra[4])],
        [(algebra[0], algebra[1]), (diag_one, zeros_like), (algebra[5], -algebra[6])],
        [(algebra[3], algebra[4]), (algebra[5], algebra[6]), (diag_two, zeros_like)],
    ]
    generator = [[(-half_step * h[1], half_step * h[0]) for h in row] for row in hermitian]
    square = matrix_mul(generator[:2], generator)
    rows_two = []
    for i in range(2):
        entries = []
        for j in range(3):
            real_value = generator[i][j][0] + 0.5 * square[i][j][0]
            if i == j:
                real_value = real_value + 1.0
            entries.append((real_value, generator[i][j][1] + 0.5 * square[i][j][1]))
        rows_two.append(entries)
    length = jnp.sqrt(sum((p[0] * p[0] + p[1] * p[1] for p in rows_two[0])))
    row_one = [(p[0] / length, p[1] / length) for p in rows_two[0]]
    correlation = complex_mul(complex_conj(row_one[0]), rows_two[1][0])
    for k in (1, 2):
        correlation = complex_add(
            correlation, complex_mul(complex_conj(row_one[k]), rows_two[1][k])
        )
    row_two = [complex_sub(rows_two[1][k], complex_mul(correlation, row_one[k])) for k in range(3)]
    length = jnp.sqrt(sum((p[0] * p[0] + p[1] * p[1] for p in row_two)))
    row_two = [(p[0] / length, p[1] / length) for p in row_two]
    return [row_one, row_two, cross_conj(row_one, row_two)]


def two_rows(product, axis):
    return jnp.stack(
        [
            jnp.stack([jnp.stack(product[r][c], axis=axis) for c in range(3)], axis=axis)
            for r in range(2)
        ],
        axis=axis,
    )


def matrix_stack(matrix):
    return jnp.stack([jnp.stack([jnp.stack(matrix[i][j]) for j in range(3)]) for i in range(3)])


def matrix_from(stacked):
    return [[(stacked[i, j, 0], stacked[i, j, 1]) for j in range(3)] for i in range(3)]


def plane_step(values, einsum_form, cosine_table, sine_table, sign_value, pair_count):
    highest = lax.Precision.HIGHEST
    with_cos = jnp.einsum(einsum_form, values, cosine_table, precision=highest)
    with_sin = jnp.einsum(einsum_form, values, sine_table, precision=highest)
    dims_shape = with_cos.shape
    with_cos = with_cos.reshape(dims_shape[0], dims_shape[1], pair_count, 2, -1)
    with_sin = with_sin.reshape(dims_shape[0], dims_shape[1], pair_count, 2, -1)
    real_out = with_cos[:, :, :, 0] - sign_value * with_sin[:, :, :, 1]
    imag_out = with_cos[:, :, :, 1] + sign_value * with_sin[:, :, :, 0]
    return jnp.stack([real_out, imag_out], axis=3).reshape(dims_shape)


def body(links):
    highest = lax.Precision.HIGHEST
    extent = EXTENT
    slices = links.shape[0]
    local_sites = links.shape[-1]
    plane_size = extent * extent
    lower_width = (extent - 1) * extent
    rows_dev = local_sites // extent
    device = lax.axis_index("space")
    site_index = jnp.arange(local_sites, dtype=jnp.int32)
    xcoord = site_index % extent
    zcoord = (device * rows_dev + site_index // extent - storage_offset) % extent
    along_x = links[:, 0]
    along_y = links[:, 1]
    along_z = links[:, 2]
    below_piece = jnp.concatenate(
        [along_y[..., local_sites - plane_size :], along_z[..., local_sites - extent :]], axis=-1
    )
    from_below = from_behind(below_piece, "space", 1)
    from_above = from_behind(along_z[..., : plane_size - extent], "space", -1)
    behind_x = jnp.where(
        xcoord == 0, jnp.roll(along_x, -(extent - 1), axis=-1), jnp.roll(along_x, 1, axis=-1)
    )
    behind_y = jnp.concatenate(
        [from_below[..., :plane_size], along_y[..., : local_sites - plane_size]], axis=-1
    )
    near_z = jnp.concatenate(
        [from_below[..., plane_size:], along_z[..., : local_sites - extent]], axis=-1
    )
    wrap_z = jnp.concatenate([along_z[..., plane_size - extent :], from_above], axis=-1)
    behind_z = jnp.where(zcoord == 0, wrap_z, near_z)
    current = [link_matrix(along_x), link_matrix(along_y), link_matrix(along_z)]
    behind = [link_matrix(behind_x), link_matrix(behind_y), link_matrix(behind_z)]
    algebra = algebra_of(gradient_of(current, behind))
    theta_part = sum((jnp.sum(a * a) for a in algebra))
    theta_total = lax.psum(theta_part, ("tm", "space"))
    wave_number = jnp.arange(extent, dtype=jnp.int32)
    angle_table = (
        2.0
        * math.pi
        / extent
        * (wave_number[:, None] * wave_number[None, :] % extent).astype(jnp.float32)
    )
    cosine_table = jnp.cos(angle_table)
    sine_table = jnp.sin(angle_table)
    fields = jnp.stack(algebra).reshape(8, slices, rows_dev, extent)
    paired = fields.reshape(4, 2, slices, rows_dev, extent)
    even_part = paired[:, 0]
    odd_part = paired[:, 1]
    real_x = jnp.einsum("csqx,kx->qcks", even_part, cosine_table, precision=highest)
    real_x = real_x + jnp.einsum("csqx,kx->qcks", odd_part, sine_table, precision=highest)
    imag_x = jnp.einsum("csqx,kx->qcks", odd_part, cosine_table, precision=highest)
    imag_x = imag_x - jnp.einsum("csqx,kx->qcks", even_part, sine_table, precision=highest)
    packed = jnp.stack([real_x, imag_x], axis=3).reshape(rows_dev, 4 * extent * 2 * slices)
    planes = lax.all_to_all(packed, "space", split_axis=1, concat_axis=0, tiled=True)
    pair_count = planes.shape[1] // (2 * slices)
    planes = jnp.roll(planes, -storage_offset, axis=0)
    planes = planes.reshape(extent, extent, planes.shape[1])
    planes = plane_step(planes, "yzc,kz->ykc", cosine_table, sine_table, -1.0, pair_count)
    planes = plane_step(planes, "yzc,ky->kzc", cosine_table, sine_table, -1.0, pair_count)
    pair_kx = (device * pair_count + jnp.arange(pair_count, dtype=jnp.int32)) % extent
    wave_term = 4.0 * jnp.sin(math.pi * wave_number.astype(jnp.float32) / extent) ** 2
    wave_pair = 4.0 * jnp.sin(math.pi * pair_kx.astype(jnp.float32) / extent) ** 2
    momentum = wave_term[:, None, None] + wave_term[None, :, None] + wave_pair[None, None, :]
    zero_mode = (
        wave_number[:, None, None] + wave_number[None, :, None] + pair_kx[None, None, :] == 0
    )
    factor = jnp.where(
        zero_mode, 0.0, top_momentum / (extent**3 * jnp.where(zero_mode, 1.0, momentum))
    )
    planes = (
        planes.reshape(extent, extent, pair_count, 2 * slices) * factor[:, :, :, None]
    ).reshape(extent, extent, -1)
    planes = plane_step(planes, "yzc,kz->ykc", cosine_table, sine_table, 1.0, pair_count)
    planes = plane_step(planes, "yzc,ky->kzc", cosine_table, sine_table, 1.0, pair_count)
    planes = jnp.roll(planes.reshape(plane_size, -1), storage_offset, axis=0)
    returned = lax.all_to_all(planes, "space", split_axis=0, concat_axis=1, tiled=True)
    returned = returned.reshape(rows_dev, 4, extent, 2, slices)
    real_back = returned[:, :, :, 0]
    imag_back = returned[:, :, :, 1]
    even_smooth = jnp.einsum("qcks,kx->csqx", real_back, cosine_table, precision=highest)
    even_smooth = even_smooth - jnp.einsum(
        "qcks,kx->csqx", imag_back, sine_table, precision=highest
    )
    odd_smooth = jnp.einsum("qcks,kx->csqx", real_back, sine_table, precision=highest)
    odd_smooth = odd_smooth + jnp.einsum(
        "qcks,kx->csqx", imag_back, cosine_table, precision=highest
    )
    smooth = jnp.stack([even_smooth, odd_smooth], axis=1).reshape(8, slices, local_sites)
    rotation = rotation_of([smooth[a] for a in range(8)])
    stacked = matrix_stack(rotation)
    upper_rim = from_behind(stacked[..., :plane_size], "space", -1)
    lower_rim = from_behind(stacked[..., local_sites - lower_width :], "space", 1)
    wide_rot = matrix_from(jnp.concatenate([lower_rim, stacked, upper_rim], axis=-1))
    ahead_x = jax.tree.map(
        lambda a: jnp.where(
            xcoord == extent - 1, jnp.roll(a, extent - 1, axis=-1), jnp.roll(a, -1, axis=-1)
        ),
        rotation,
    )
    ahead_y = jax.tree.map(
        lambda a: a[..., lower_width + plane_size : lower_width + plane_size + local_sites],
        wide_rot,
    )
    ahead_z = jax.tree.map(
        lambda a: jnp.where(
            zcoord == extent - 1,
            a[..., :local_sites],
            a[..., lower_width + extent : lower_width + extent + local_sites],
        ),
        wide_rot,
    )
    ahead_all = [ahead_x, ahead_y, ahead_z]
    new_dirs = []
    deficit_part = jnp.zeros((slices,), jnp.float32)
    for d in range(3):
        product = matrix_mul(matrix_mul(rotation, current[d]), dagger_of(ahead_all[d]))
        deficit_part = deficit_part + jnp.sum(
            3.0 - product[0][0][0] - product[1][1][0] - product[2][2][0], axis=-1
        )
        new_dirs.append(two_rows(product, 1))
    new_links = jnp.stack(new_dirs, axis=1)
    deficit_total = lax.psum(deficit_part, "space")
    theta = theta_total / (slices * lax.axis_size("tm") * extent**3)
    deficit = deficit_total / extent**3
    return (new_links, theta, deficit)


def solution(mesh):
    placed = (P("tm", None, None, None, None, "space"),)
    return jax.shard_map(
        body,
        mesh=mesh,
        in_specs=placed,
        out_specs=(P("tm", None, None, None, None, "space"), P(), P("tm")),
        check_vma=False,
    )
```

profile of v0, /device:TPU:0, one launch (start us, length us, event | category | flops | bytes accessed | tf_op | source)
XLA Modules:
  0.0 408.8 jit_solution(4929725969459849419)
XLA Ops:
  0.6 3.5 fusion.979
  5.2 6.4 %collective-permute-start.1 = (f32[8,2,3,2,2256]{4,0,3,2,1:T(8,128)}, f32[8,2,3,2,2256]{4,0,3,2,1:T(8,128)}, u32[]{:S(2)}, u32[]{:S(2)}) collective-permute-start(f32[8,2,3,2,2256]{4,0,3,2,1:T(8,128)} %slice.1086), channel_id=1, source_target_pairs={{1,0},{2,1},{3,2},{4,3},{5,4},{6,5},{7,6},{8,7},{9,8},{10,9},{11,1... | collective-permute-start | bytes 2598920 | tf_op jit(solution)/shard_map/ppermute | solution.py:20
  14.1 1.5 slice.1072
  15.8 1.7 maximum_select_fusion
  17.5 12.5 %collective-permute-done = f32[8,2,3,2,2352]{4,0,3,2,1:T(8,128)} collective-permute-done((f32[8,2,3,2,2352]{4,0,3,2,1:T(8,128)}, f32[8,2,3,2,2352]{4,0,3,2,1:T(8,128)}, u32[]{:S(2)}, u32[]{:S(2)}) %collective-permute-start) | collective-permute-done | bytes 903200 | tf_op jit(solution)/shard_map/ppermute | solution.py:20
  32.1 1.9 maximum_select_fusion.1
  42.9 3.7 reshape_reshape.9
  46.6 4.7 %fusion.9 = f32[48,4,8,72]{3,0,2,1:T(8,128)S(1)} fusion(f32[4,2,8,72,48]{4,3,2,1,0:T(8,128)} %reshape_reshape.9), kind=kOutput, calls=%fused_computation.67 | convolution fusion | flops 63721728 | bytes 1622016 | tf_op jit(solution)/shard_map/csqx,kx->qcks/dot_general | solution.py:217
  51.4 4.6 %fusion.8 = f32[48,4,8,72]{3,0,2,1:T(8,128)S(1)} fusion(f32[4,2,8,72,48]{4,3,2,1,0:T(8,128)} %reshape_reshape.9), kind=kOutput, calls=%fused_computation.66 | convolution fusion | flops 63721728 | bytes 1622016 | tf_op jit(solution)/shard_map/csqx,kx->qcks/dot_general | solution.py:215
  56.0 3.3 fusion.2
  59.3 3.3 fusion.3
  62.7 1.6 copy.285
  64.4 2.9 copy.286
  67.3 6.0 %all-to-all-start = ((f32[72,32,96]{2,0,1:T(8,128)}), f32[72,32,96]{2,0,1:T(8,128)}, u32[]{:S(2)}, u32[]{:S(2)}) async-start(f32[72,32,96]{2,0,1:T(8,128)} %copy.286), calls=%async_computation | async-start | bytes 2359296 | tf_op jit(solution)/shard_map/all_to_all | solution.py:220
  73.7 1.6 mul.13989
  75.3 2.8 copy.300
  78.1 24.2 %all-to-all-done = f32[72,32,96]{2,0,1:T(8,128)} async-done(((f32[72,32,96]{2,0,1:T(8,128)}), f32[72,32,96]{2,0,1:T(8,128)}, u32[]{:S(2)}, u32[]{:S(2)}) %all-to-all-start) | async-done | bytes 884768 | tf_op jit(solution)/shard_map/all_to_all | solution.py:220
  103.0 1.3 slice.1168
  104.4 2.3 convolution_bitcast_fusion.2
  106.7 2.3 convolution_bitcast_fusion.3
  109.0 2.9 copy.357
  111.9 2.9 copy.355
  114.8 2.6 fusion.7
  117.4 1.6 pad_maximum_fusion.1
  119.0 3.1 copy.295
  122.1 10.3 %fusion.728 = f32[48,48,6,2,8]{1,0,4,3,2:T(8,128)S(1)} fusion(f32[48,6,2,8,48]{4,0,3,2,1:T(8,128)} %bitcast.4454), kind=kOutput, calls=%fused_computation.1642 | convolution fusion | flops 127422720 | bytes 1769472 | tf_op jit(solution)/shard_map/yzc,ky->kzc/dot_general | solution.py:157
  132.5 8.5 %fusion.738 = f32[48,48,6,2,8]{1,0,4,3,2:T(8,128)S(1)} fusion(f32[48,6,2,8,48]{4,0,3,2,1:T(8,128)S(1)} %bitcast.4455), kind=kOutput, calls=%fused_computation.1652 | convolution fusion | flops 127422720 | bytes 1769472 | tf_op jit(solution)/shard_map/yzc,ky->kzc/dot_general | solution.py:156
  141.2 1.6 pad_maximum_fusion.2
  142.8 3.2 copy.299
  146.1 4.1 convolution_bitcast_fusion
  150.1 2.3 convolution_bitcast_fusion.1
  152.4 2.8 copy.304
  155.3 2.9 copy.302
  158.2 2.6 slice_subtract_fusion.1
  160.8 1.6 pad_maximum_fusion.3
  162.5 3.2 copy.305
  165.7 10.3 %fusion.726 = f32[48,48,6,2,8]{1,0,4,3,2:T(8,128)S(1)} fusion(f32[48,6,2,8,48]{4,0,3,2,1:T(8,128)} %bitcast.4456), kind=kOutput, calls=%fused_computation.1640 | convolution fusion | flops 127422720 | bytes 1769472 | tf_op jit(solution)/shard_map/yzc,ky->kzc/dot_general | solution.py:157
  176.0 8.5 %fusion.740 = f32[48,48,6,2,8]{1,0,4,3,2:T(8,128)S(1)} fusion(f32[48,6,2,8,48]{4,0,3,2,1:T(8,128)S(1)} %bitcast.4457), kind=kOutput, calls=%fused_computation.1654 | convolution fusion | flops 127422720 | bytes 1769472 | tf_op jit(solution)/shard_map/yzc,ky->kzc/dot_general | solution.py:156
  184.8 1.6 pad_maximum_fusion.4
  186.4 2.4 reshape_reshape.11
  189.5 1.4 copy.371
  191.8 2.4 pad_maximum_fusion.9
  194.2 3.7 all-to-all-start.1
  199.9 27.1 %all-to-all-done.1 = f32[32,72,96]{2,1,0:T(8,128)} async-done(((f32[32,72,96]{2,1,0:T(8,128)}), f32[32,72,96]{2,1,0:T(8,128)}, u32[]{:S(2)}, u32[]{:S(2)}) %all-to-all-start.1) | async-done | bytes 884768 | tf_op jit(solution)/shard_map/all_to_all | solution.py:242
  227.0 2.9 copy.310
  229.9 1.5 fusion.980
  235.0 1.3 pad_maximum_fusion.7
  236.4 2.9 copy.313
  239.3 2.3 reshape.11989
  254.7 5.3 %collective-permute-start.3 = (f32[3,3,2,8,2304]{4,3,2,1,0:T(8,128)S(1)}, f32[3,3,2,8,2304]{4,3,2,1,0:T(8,128)}, u32[]{:S(2)}, u32[]{:S(2)}) collective-permute-start(f32[3,3,2,8,2304]{4,3,2,1,0:T(8,128)S(1)} %slice.1271), channel_id=1, source_target_pairs={{1,0},{2,1},{3,2},{4,3},{5,4},{6,5},{7,6},{8,7},{9,8},{10,9},{11,1... | collective-permute-start | bytes 3981320 | tf_op jit(solution)/shard_map/ppermute | solution.py:20
  263.7 11.9 %collective-permute-done.2 = f32[3,3,2,8,2256]{4,3,2,1,0:T(8,128)} collective-permute-done((f32[3,3,2,8,2256]{4,3,2,1,0:T(8,128)S(1)}, f32[3,3,2,8,2256]{4,3,2,1,0:T(8,128)}, u32[]{:S(2)}, u32[]{:S(2)}) %collective-permute-start.2) | collective-permute-done | bytes 1299488 | tf_op jit(solution)/shard_map/ppermute | solution.py:20
  275.7 6.6 %concatenate.1157 = f32[3,3,2,8,8016]{4,3,2,1,0:T(8,128)} concatenate(f32[3,3,2,8,2256]{4,3,2,1,0:T(8,128)} %collective-permute-done.2, f32[3,3,2,8,3456]{4,3,2,1,0:T(8,128)} %copy-done.7, f32[3,3,2,8,2304]{4,3,2,1,0:T(8,128)} %collective-permute-done.3), dimensions={4} | concatenate | bytes 9234432 | tf_op jit(solution)/shard_map/concatenate | solution.py:259
  282.4 2.9 slice_bitcast_fusion.17
  285.5 2.9 fusion.706
  320.3 2.8 fusion.707
  328.7 1.3 maximum_bitcast_fusion
  333.0 2.5 fusion.170
  336.1 2.5 fusion.177
  339.2 2.6 fusion.95
  342.3 2.4 fusion.102
  346.3 2.7 pad_maximum_fusion
  349.5 3.4 fusion.708
  353.5 4.0 copy.332
  357.5 48.7 %all-reduce = (f32[]{:T(128)}, f32[8]{0:T(128)S(1)}) all-reduce(f32[]{:T(128)S(6)} %add.9190, f32[8]{0:T(128)S(1)} %add_add_fusion.11), channel_id=1, replica_groups=mesh['tm'=1,'space'=32] {'tm','space'}, use_global_device_ids=true, to_apply=%region_8.9 | all-reduce | flops 9 | bytes 72 | tf_op jit(solution)/shard_map/psum | solution.py:201
  (426 shorter events, 79.8 us)
Async XLA Ops:
  5.2 26.8 %collective-permute-start.1 = (f32[8,2,3,2,2256]{4,0,3,2,1:T(8,128)}, f32[8,2,3,2,2256]{4,0,3,2,1:T(8,128)}, u32[]{:S(2)}, u32[]{:S(2)}) collective-permute-start(f32[8,2,3,2,2256]{4,0,3,2,1:T(8,128)} %slice.1086), channel_id=1, source_target_pairs={{1,0},{2,1},{3,2},{4,3},{5,4},{6,5},{7,6},{8,7},{9,8},{10,9},{11,1... | collective-permute-start | bytes 2598920 | tf_op jit(solution)/shard_map/ppermute | solution.py:20
  11.8 3.9 copy-start.4
  13.0 17.0 %collective-permute-start = (f32[8,2,3,2,2352]{4,0,3,2,1:T(8,128)}, f32[8,2,3,2,2352]{4,0,3,2,1:T(8,128)}, u32[]{:S(2)}, u32[]{:S(2)}) collective-permute-start(f32[8,2,3,2,2352]{4,0,3,2,1:T(8,128)} %pad_maximum_fusion.10), channel_id=1, source_target_pairs={{31,0},{0,1},{1,2},{2,3},{3,4},{4,5},{5,6},{6,7},{7,8},{8,9},{9,10... | collective-permute-start | bytes 2709512 | tf_op jit(solution)/shard_map/ppermute | solution.py:20
  17.5 24.3 %copy-start = (f32[8,2,3,2,3456]{4,0,3,2,1:T(8,128)}, f32[8,2,3,2,3456]{4,0,3,2,1:T(8,128)S(1)}, u32[]{:S(2)}) copy-start(f32[8,2,3,2,3456]{4,0,3,2,1:T(8,128)S(1)} %maximum_select_fusion) | copy-start | bytes 3981316
  17.5 14.5 %copy-start.91 = (f32[8,2,3,2,1200]{4,0,3,2,1:T(8,128)S(1)}, f32[8,2,3,2,1200]{4,0,3,2,1:T(8,128)}, u32[]{:S(2)}) copy-start(f32[8,2,3,2,1200]{4,0,3,2,1:T(8,128)} %slice.1085) | copy-start | bytes 1382404
  34.0 7.8 %copy-start.2 = (f32[8,2,3,2,3456]{4,0,3,2,1:T(8,128)}, f32[8,2,3,2,3456]{4,0,3,2,1:T(8,128)S(1)}, u32[]{:S(2)}) copy-start(f32[8,2,3,2,3456]{4,0,3,2,1:T(8,128)S(1)} %maximum_select_fusion.1) | copy-start | bytes 3981316
  34.9 7.0 %copy-start.13 = (f32[8,1,1,1,3456]{4,0,3,2,1:T(8,128)}, f32[8,1,1,1,3456]{4,0,3,2,1:T(8,128)S(1)}, u32[]{:S(2)}) copy-start(f32[8,1,1,1,3456]{4,0,3,2,1:T(8,128)S(1)} %get-tuple-element.94) | copy-start | bytes 331780
  34.9 7.0 %copy-start.17 = (f32[8,1,1,1,3456]{4,0,3,2,1:T(8,128)}, f32[8,1,1,1,3456]{4,0,3,2,1:T(8,128)S(1)}, u32[]{:S(2)}) copy-start(f32[8,1,1,1,3456]{4,0,3,2,1:T(8,128)S(1)} %get-tuple-element.93) | copy-start | bytes 331780
  35.6 6.3 %copy-start.15 = (f32[8,1,1,1,3456]{4,0,3,2,1:T(8,128)}, f32[8,1,1,1,3456]{4,0,3,2,1:T(8,128)S(1)}, u32[]{:S(2)}) copy-start(f32[8,1,1,1,3456]{4,0,3,2,1:T(8,128)S(1)} %get-tuple-element.91) | copy-start | bytes 331780
  35.6 6.3 %copy-start.19 = (f32[8,1,1,1,3456]{4,0,3,2,1:T(8,128)}, f32[8,1,1,1,3456]{4,0,3,2,1:T(8,128)S(1)}, u32[]{:S(2)}) copy-start(f32[8,1,1,1,3456]{4,0,3,2,1:T(8,128)S(1)} %get-tuple-element.90) | copy-start | bytes 331780
  37.8 4.1 copy-start.47
  37.8 4.1 %copy-start.50 = (f32[8,1,1,1,3456]{4,0,3,2,1:T(8,128)}, f32[8,1,1,1,3456]{4,0,3,2,1:T(8,128)S(1)}, u32[]{:S(2)}) copy-start(f32[8,1,1,1,3456]{4,0,3,2,1:T(8,128)S(1)} %get-tuple-element.230) | copy-start | bytes 331780
  38.8 3.1 copy-start.55
  46.6 9.3 %copy-start.10 = (f32[4,2,8,72,48]{4,3,2,1,0:T(8,128)S(1)}, f32[4,2,8,72,48]{4,3,2,1,0:T(8,128)}, u32[]{:S(2)}) copy-start(f32[4,2,8,72,48]{4,3,2,1,0:T(8,128)} %reshape_reshape.9) | copy-start | bytes 2654212
  67.3 35.0 %all-to-all-start = ((f32[72,32,96]{2,0,1:T(8,128)}), f32[72,32,96]{2,0,1:T(8,128)}, u32[]{:S(2)}, u32[]{:S(2)}) async-start(f32[72,32,96]{2,0,1:T(8,128)} %copy.286), calls=%async_computation | async-start | bytes 2359296 | tf_op jit(solution)/shard_map/all_to_all | solution.py:220
  122.1 10.3 %copy-start.8 = (f32[48,48,96]{0,1,2:T(8,128)S(1)}, f32[48,48,96]{0,1,2:T(8,128)}, u32[]{:S(2)}) copy-start(f32[48,48,96]{0,1,2:T(8,128)} %copy.295) | copy-start | bytes 2654212
  146.1 4.1 %copy-start.11 = (f32[48,48,96]{2,1,0:T(8,128)S(1)}, f32[48,48,96]{2,1,0:T(8,128)}, u32[]{:S(2)}) copy-start(f32[48,48,96]{2,1,0:T(8,128)} %copy.300) | copy-start | bytes 2654212
  146.1 4.1 copy-start.12
  165.7 10.3 %copy-start.9 = (f32[48,96,48]{2,0,1:T(8,128)S(1)}, f32[48,96,48]{2,0,1:T(8,128)}, u32[]{:S(2)}) copy-start(f32[48,96,48]{2,0,1:T(8,128)} %copy.305) | copy-start | bytes 2654212
  194.2 32.8 %all-to-all-start.1 = ((f32[32,72,96]{2,1,0:T(8,128)}), f32[32,72,96]{2,1,0:T(8,128)}, u32[]{:S(2)}, u32[]{:S(2)}) async-start(f32[32,72,96]{2,1,0:T(8,128)} %bitcast.4470), calls=%async_computation.1 | async-start | bytes 2359296 | tf_op jit(solution)/shard_map/all_to_all | solution.py:242
  245.7 16.9 %copy-start.29 = (f32[8,3456]{1,0:T(8,128)}, f32[8,3456]{1,0:T(8,128)S(1)}, u32[]{:S(2)}) copy-start(f32[8,3456]{1,0:T(8,128)S(1)} %get-tuple-element.199) | copy-start | bytes 331780
  245.7 16.9 %copy-start.32 = (f32[8,3456]{1,0:T(8,128)}, f32[8,3456]{1,0:T(8,128)S(1)}, u32[]{:S(2)}) copy-start(f32[8,3456]{1,0:T(8,128)S(1)} %get-tuple-element.200) | copy-start | bytes 331780
  245.7 16.9 %copy-start.35 = (f32[8,3456]{1,0:T(8,128)}, f32[8,3456]{1,0:T(8,128)S(1)}, u32[]{:S(2)}) copy-start(f32[8,3456]{1,0:T(8,128)S(1)} %get-tuple-element.201) | copy-start | bytes 331780
  245.7 16.9 %copy-start.38 = (f32[8,3456]{1,0:T(8,128)}, f32[8,3456]{1,0:T(8,128)S(1)}, u32[]{:S(2)}) copy-start(f32[8,3456]{1,0:T(8,128)S(1)} %get-tuple-element.203) | copy-start | bytes 331780
  245.7 16.9 %copy-start.41 = (f32[8,3456]{1,0:T(8,128)}, f32[8,3456]{1,0:T(8,128)S(1)}, u32[]{:S(2)}) copy-start(f32[8,3456]{1,0:T(8,128)S(1)} %get-tuple-element.205) | copy-start | bytes 331780
  245.7 16.9 %copy-start.44 = (f32[8,3456]{1,0:T(8,128)}, f32[8,3456]{1,0:T(8,128)S(1)}, u32[]{:S(2)}) copy-start(f32[8,3456]{1,0:T(8,128)S(1)} %get-tuple-element.208) | copy-start | bytes 331780
  254.6 21.1 %collective-permute-start.2 = (f32[3,3,2,8,2256]{4,3,2,1,0:T(8,128)S(1)}, f32[3,3,2,8,2256]{4,3,2,1,0:T(8,128)}, u32[]{:S(2)}, u32[]{:S(2)}) collective-permute-start(f32[3,3,2,8,2256]{4,3,2,1,0:T(8,128)S(1)} %slice.1270), channel_id=1, source_target_pairs={{31,0},{0,1},{1,2},{2,3},{3,4},{4,5},{5,6},{6,7},{7,8},{8,9},{9,10... | collective-permute-start | bytes 3898376 | tf_op jit(solution)/shard_map/ppermute | solution.py:20
  254.7 21.0 %collective-permute-start.3 = (f32[3,3,2,8,2304]{4,3,2,1,0:T(8,128)S(1)}, f32[3,3,2,8,2304]{4,3,2,1,0:T(8,128)}, u32[]{:S(2)}, u32[]{:S(2)}) collective-permute-start(f32[3,3,2,8,2304]{4,3,2,1,0:T(8,128)S(1)} %slice.1271), channel_id=1, source_target_pairs={{1,0},{2,1},{3,2},{4,3},{5,4},{6,5},{7,6},{8,7},{9,8},{10,9},{11,1... | collective-permute-start | bytes 3981320 | tf_op jit(solution)/shard_map/ppermute | solution.py:20
  282.4 3.1 copy-start.122
  282.4 3.1 copy-start.123
  288.4 31.8 %copy-start.69 = (f32[8,3456]{1,0:T(8,128)}, f32[8,3456]{1,0:T(8,128)S(1)}, u32[]{:S(2)}) copy-start(f32[8,3456]{1,0:T(8,128)S(1)} %get-tuple-element.21) | copy-start | bytes 331780
  288.4 31.8 %copy-start.71 = (f32[8,3456]{1,0:T(8,128)}, f32[8,3456]{1,0:T(8,128)S(1)}, u32[]{:S(2)}) copy-start(f32[8,3456]{1,0:T(8,128)S(1)} %get-tuple-element.22) | copy-start | bytes 331780
  288.4 31.8 %copy-start.73 = (f32[8,3456]{1,0:T(8,128)}, f32[8,3456]{1,0:T(8,128)S(1)}, u32[]{:S(2)}) copy-start(f32[8,3456]{1,0:T(8,128)S(1)} %get-tuple-element.23) | copy-start | bytes 331780
  288.4 31.8 %copy-start.75 = (f32[8,3456]{1,0:T(8,128)}, f32[8,3456]{1,0:T(8,128)S(1)}, u32[]{:S(2)}) copy-start(f32[8,3456]{1,0:T(8,128)S(1)} %get-tuple-element.24) | copy-start | bytes 331780
  288.5 31.8 %copy-start.77 = (f32[8,3456]{1,0:T(8,128)}, f32[8,3456]{1,0:T(8,128)S(1)}, u32[]{:S(2)}) copy-start(f32[8,3456]{1,0:T(8,128)S(1)} %get-tuple-element.26) | copy-start | bytes 331780
  288.5 31.8 %copy-start.79 = (f32[8,3456]{1,0:T(8,128)}, f32[8,3456]{1,0:T(8,128)S(1)}, u32[]{:S(2)}) copy-start(f32[8,3456]{1,0:T(8,128)S(1)} %get-tuple-element.44) | copy-start | bytes 331780
  288.5 31.8 %copy-start.81 = (f32[8,3456]{1,0:T(8,128)}, f32[8,3456]{1,0:T(8,128)S(1)}, u32[]{:S(2)}) copy-start(f32[8,3456]{1,0:T(8,128)S(1)} %get-tuple-element.45) | copy-start | bytes 331780
  288.5 31.8 %copy-start.83 = (f32[8,3456]{1,0:T(8,128)}, f32[8,3456]{1,0:T(8,128)S(1)}, u32[]{:S(2)}) copy-start(f32[8,3456]{1,0:T(8,128)S(1)} %get-tuple-element.46) | copy-start | bytes 331780
  288.5 31.8 %copy-start.85 = (f32[8,3456]{1,0:T(8,128)}, f32[8,3456]{1,0:T(8,128)S(1)}, u32[]{:S(2)}) copy-start(f32[8,3456]{1,0:T(8,128)S(1)} %get-tuple-element.47) | copy-start | bytes 331780
  288.5 31.8 %copy-start.87 = (f32[8,3456]{1,0:T(8,128)}, f32[8,3456]{1,0:T(8,128)S(1)}, u32[]{:S(2)}) copy-start(f32[8,3456]{1,0:T(8,128)S(1)} %get-tuple-element.48) | copy-start | bytes 331780
  288.5 31.8 %copy-start.89 = (f32[8,3456]{1,0:T(8,128)}, f32[8,3456]{1,0:T(8,128)S(1)}, u32[]{:S(2)}) copy-start(f32[8,3456]{1,0:T(8,128)S(1)} %get-tuple-element.49) | copy-start | bytes 331780
  288.5 31.8 %copy-start.92 = (f32[8,3456]{1,0:T(8,128)}, f32[8,3456]{1,0:T(8,128)S(1)}, u32[]{:S(2)}) copy-start(f32[8,3456]{1,0:T(8,128)S(1)} %get-tuple-element.25) | copy-start | bytes 331780
  310.2 10.1 %copy-start.124 = (pred[3456]{0:T(1024)(128)(4,1)S(1)}, pred[3456]{0:T(1024)(128)(4,1)}, u32[]{:S(2)}) copy-start(pred[3456]{0:T(1024)(128)(4,1)} %broadcast_compare_fusion) | copy-start | bytes 10372
  339.2 3.2 copy-start.49
  339.2 3.2 copy-start.54
  345.9 3.1 copy-start.31
  345.9 3.1 copy-start.34
  345.9 3.1 copy-start.37
  345.9 3.1 copy-start.40
  345.9 3.1 copy-start.43
  345.9 3.1 copy-start.46
  345.9 3.1 copy-start.70
  346.0 3.1 copy-start.72
  346.0 3.1 copy-start.74
  346.0 3.1 copy-start.76
  346.0 3.1 copy-start.78
  346.0 3.1 copy-start.80
  346.0 3.1 copy-start.82
  346.0 3.1 copy-start.84
  346.2 3.1 copy-start.112
  346.2 3.1 copy-start.113
  346.3 3.1 copy-start.114
  346.3 3.2 copy-start.115
  346.3 3.2 copy-start.116
  (67 other events, 157.9 us)
where the time goes:
time: 415 us; the launch traced here: 409 us
  local copies, waits for them, and re-layouts  116 us (28%)
  waiting for transfers between devices  75.8 us (18%)
  other arithmetic  69.1 us (17%)
  matrix products  68.1 us (16%)
  blocking collectives  48.7 us (12%)
  starting transfers between devices  21.6 us (5%)
  between operations  9.56 us (2%)
    psum x1, blocking collectives, body(): theta_total = lax.psum(theta_part, ('tm', 'space'))  48.7 us
    all_to_all x1, waiting for transfers between devices, body(): lax.all_to_all(planes, 'space', split_axis=0, concat_axis=1, tiled=True)  27.1 us
    dot_general x4, matrix products, plane_step(): with_sin = jnp.einsum(einsum_form, values, sine_table, precision=highest)  26.9 us
    ppermute x4, waiting for transfers between devices, from_behind(): return lax.ppermute(block, axis, route)  24.4 us
    all_to_all x1, waiting for transfers between devices, body(): lax.all_to_all(packed, 'space', split_axis=1, concat_axis=0, tiled=True)  24.2 us
    dot_general x4, matrix products, plane_step(): with_cos = jnp.einsum(einsum_form, values, cosine_table, precision=highest)  21.5 us
    slice x30, local copies, waits for them, and re-layouts, body(): jnp.roll(a, extent - 1, axis=-1)  19.4 us
    slice x30, local copies, waits for them, and re-layouts, body(): jnp.roll(a, -1, axis=-1)  19.2 us
  transfers between devices with their start and end apart: 6, of which 4 were waited for; matrix products, arithmetic and copies ran while one was open for 4% of the time, Pallas kernels for 0%

commit v1 on v0

v1 whole, which is shorter than its diff:
```python
import functools
import math

import jax
import jax.numpy as jnp
import numpy as np
from jax import lax
from jax.experimental import pallas as pl
from jax.experimental.pallas import tpu as pltpu
from jax.sharding import PartitionSpec as P

EXTENT = 48
LANES = 128
HALF = 64
SEG = 16

root_three = math.sqrt(3.0)
step_size = 0.08
top_momentum = 12.0

f32 = jnp.float32
bf16 = jnp.bfloat16
MESH = pl.DeviceIdType.MESH
VM = pl.BlockSpec(memory_space=pltpu.VMEM)
PARAMS = pltpu.CompilerParams(vmem_limit_bytes=60 * 1024 * 1024)


def from_behind(block, axis, distance):
    n = lax.axis_size(axis)
    return lax.ppermute(block, axis, [((i - distance) % n, i) for i in range(n)])


def cmul(p, q):
    return (p[0] * q[0] - p[1] * q[1], p[0] * q[1] + p[1] * q[0])


def cadd(p, q):
    return (p[0] + q[0], p[1] + q[1])


def csub(p, q):
    return (p[0] - q[0], p[1] - q[1])


def conj(p):
    return (p[0], -p[1])


def conj_mul(p, q):
    return (p[0] * q[0] + p[1] * q[1], p[0] * q[1] - p[1] * q[0])


def mul_conj(p, q):
    return (p[0] * q[0] + p[1] * q[1], p[1] * q[0] - p[0] * q[1])


def dot_row(row, col, mul):
    out = mul(row[0], col[0])
    for k in (1, 2):
        out = cadd(out, mul(row[k], col[k]))
    return out


def cross_conj(a, b):
    return [
        conj(csub(cmul(a[(k + 1) % 3], b[(k + 2) % 3]), cmul(a[(k + 2) % 3], b[(k + 1) % 3])))
        for k in range(3)
    ]


def algebra_of(u):
    return [
        u[0][1][1] + u[1][0][1],
        u[0][1][0] - u[1][0][0],
        u[0][0][1] - u[1][1][1],
        u[0][2][1] + u[2][0][1],
        u[0][2][0] - u[2][0][0],
        u[1][2][1] + u[2][1][1],
        u[1][2][0] - u[2][1][0],
        (u[0][0][1] + u[1][1][1] - 2.0 * u[2][2][1]) * (1.0 / root_three),
    ]


def rotation_of(s):
    h = 0.5 * step_size
    s = [v * h for v in s]
    third = s[7] * (1.0 / root_three)
    d0, d1, d2 = s[2] + third, third - s[2], -2.0 * third
    herm = [
        [(d0, None), (s[0], -s[1]), (s[3], -s[4])],
        [(s[0], s[1]), (d1, None), (s[5], -s[6])],
        [(s[3], s[4]), (s[5], s[6]), (d2, None)],
    ]

    def mul(p, q):
        if p[1] is None and q[1] is None:
            return (p[0] * q[0], jnp.zeros_like(p[0]))
        if p[1] is None:
            return (p[0] * q[0], p[0] * q[1])
        if q[1] is None:
            return (p[0] * q[0], p[1] * q[0])
        return cmul(p, q)

    rows = []
    for i in range(2):
        row = []
        for j in range(3):
            sq = dot_row(herm[i], [herm[k][j] for k in range(3)], mul)
            re, im = -0.5 * sq[0], -0.5 * sq[1]
            if herm[i][j][1] is not None:
                re = re - herm[i][j][1]
            else:
                re = re + 1.0
            row.append((re, im + herm[i][j][0]))
        rows.append(row)

    def unit(row):
        inv = lax.rsqrt(sum(p[0] * p[0] + p[1] * p[1] for p in row))
        return [(p[0] * inv, p[1] * inv) for p in row]

    one = unit(rows[0])
    corr = dot_row(one, rows[1], conj_mul)
    two = unit([csub(rows[1][k], cmul(corr, one[k])) for k in range(3)])
    return [one, two, cross_conj(one, two)]


def block(k):
    return pl.ds(pl.multiple_of(k * LANES, LANES), LANES)


def lane_ids(rows=8):
    return lax.broadcasted_iota(jnp.int32, (rows, LANES), 1)


def load_link(ref, d, sl):
    rows = [[(ref[d, r, c, 0, :, sl], ref[d, r, c, 1, :, sl]) for c in range(3)] for r in range(2)]
    return rows + [cross_conj(rows[0], rows[1])]


def algebra_kernel(links, out):
    def step(k, carry):
        sl = block(k)
        for d in range(3):
            for a, v in enumerate(algebra_of(load_link(links, d, sl))):
                out[d, a, :, sl] = v
        return carry

    lax.fori_loop(0, links.shape[-1] // LANES, step, 0)


def split3(x):
    hi = x.astype(bf16)
    lo = (x - hi.astype(f32)).astype(bf16)
    return jnp.concatenate([hi, lo, hi], axis=0)


def transform(table, parts, sign):
    n = parts[0].shape[0]
    both = jnp.dot(table, split3(jnp.concatenate(parts, axis=1)), preferred_element_type=f32)
    outs = []
    for i in range(len(parts)):
        mine = both[:, i * LANES : (i + 1) * LANES]
        swapped = pltpu.roll(mine[n:], HALF, 1)
        outs.append(mine[:n] + jnp.where(lane_ids(n) < HALF, sign, -sign) * swapped)
    return outs


def spread_kernel(extent, head, nsplit, alg, y_rim, z_below, z_above, coords, table, out, theta, mat, rows, freq):
    nb = alg.shape[-1] // LANES
    yb = y_rim.shape[-1] // LANES
    qh = head // extent
    hb = head // LANES
    lane = lane_ids()
    mat[...] = jnp.zeros_like(mat)

    def step(k, total):
        sl = block(k)
        before = block(jnp.maximum(k - 1, 0))
        after = block(jnp.minimum(k + 1, nb - 1))
        edge_x = coords[0, :, sl] == 0
        edge_z = coords[1, :, sl] == 0
        second = (k >= hb).astype(jnp.int32)
        dst = block(k - second * hb)
        for a in range(8):
            x, y, z = alg[0, a, :, sl], alg[1, a, :, sl], alg[2, a, :, sl]
            near = pltpu.roll(jnp.where(lane == LANES - 1, alg[0, a, :, before], x), 1, 1)
            far = pltpu.roll(jnp.where(lane < extent - 1, alg[0, a, :, after], x), LANES - extent + 1, 1)
            bx = jnp.where(edge_x, far, near)
            by = jnp.where(
                k < yb,
                y_rim[a, :, block(jnp.minimum(k, yb - 1))],
                alg[1, a, :, block(jnp.maximum(k - yb, 0))],
            )
            prev = jnp.where(k == 0, z_below[a], alg[2, a, :, before])
            near = pltpu.roll(jnp.where(lane >= LANES - extent, prev, z), extent, 1)
            far = pltpu.roll(jnp.where(k == 0, alg[2, a, :, block(yb)], z_above[a]), extent, 1)
            bz = jnp.where(edge_z, far, near)
            b = (bx - x) + (by - y) + (bz - z)
            total = total + b * b
            mat[pl.ds(pl.multiple_of((a % 2) * HALF + second * (HALF // 2) + (a // 2) * 8, 8), 8), dst] = b
        return total

    theta[...] = lax.fori_loop(0, nb, step, jnp.zeros((8, LANES), f32))
    for k in range(hb):
        rows[k * LANES : (k + 1) * LANES, :] = mat[:, k * LANES : (k + 1) * LANES].T

    def dft(i, carry):
        parts = [rows[pl.ds(pl.multiple_of((2 * i + e) * extent, 8), extent), :] for e in range(2)]
        for e, v in enumerate(transform(table[...], parts, 1.0)):
            freq[pl.ds(pl.multiple_of((2 * i + e) * extent, 8), extent), :] = v
        return carry

    lax.fori_loop(0, qh // 2, dft, 0, unroll=2)
    count = extent // (out.shape[0] // nsplit)
    q = out.shape[1]
    seg = lax.rem(lane_ids(qh), HALF) // SEG

    def pack(j, carry):
        vals = [freq[pl.ds(j * count + m, qh, stride=extent), :] for m in range(count)]
        for c in range(nsplit):
            for h in range(2):
                acc = jnp.zeros((qh, LANES), f32)
                for m in range(count):
                    moved = pltpu.roll(vals[m], ((m - (2 * h + c)) * SEG) % LANES, 1)
                    acc = jnp.where(seg == m, moved, acc)
                lo, hi = (0, qh) if h == 0 else (qh, q)
                out[j * nsplit + c, lo:hi, :] = acc[: hi - lo]
        return carry

    lax.fori_loop(0, out.shape[0] // nsplit, pack, 0)


def plane_kernel(extent, planes, wave, wave_lane, table, out, one, two):
    n = extent
    total = n * n
    scale = top_momentum / float(n) ** 3
    for y in range(n - 1):
        one[y * n : (y + 1) * n, :] = planes[y * n + 1 : (y + 1) * n + 1, :]
    one[total - n : total - 1, :] = planes[total - n + 1 : total, :]
    one[total - 1 : total, :] = planes[0:1, :]

    def rows_at(i):
        return pl.ds(pl.multiple_of(i * n, 8), n)

    def along_z(i, carry):
        parts = [one[rows_at(2 * i + e), :] for e in range(2)]
        for e, v in enumerate(transform(table[...], parts, 1.0)):
            two[rows_at(2 * i + e), :] = v
        return carry

    lax.fori_loop(0, n // 2, along_z, 0, unroll=2)

    def along_y(i, carry):
        parts = [two[pl.ds(2 * i + e, n, stride=n), :] for e in range(2)]
        vals = transform(table[...], parts, 1.0)
        done = []
        for e, v in enumerate(vals):
            p2 = wave[...] + (wave_lane[...] + wave[pl.ds(2 * i + e, 1), :])
            zero = p2 == 0.0
            done.append(v * jnp.where(zero, 0.0, scale / jnp.where(zero, 1.0, p2)))
        for e, v in enumerate(transform(table[...], done, -1.0)):
            one[rows_at(2 * i + e), :] = v
        return carry

    lax.fori_loop(0, n // 2, along_y, 0, unroll=2)

    def back_z(i, carry):
        parts = [one[pl.ds(2 * i + e, n, stride=n), :] for e in range(2)]
        for e, v in enumerate(transform(table[...], parts, -1.0)):
            two[rows_at(2 * i + e), :] = v
        return carry

    lax.fori_loop(0, n // 2, back_z, 0, unroll=2)
    out[0:1, :] = two[total - 1 : total, :]
    for y in range(n - 1):
        out[y * n + 1 : (y + 1) * n + 1, :] = two[y * n : (y + 1) * n, :]
    out[total - n + 1 : total, :] = two[total - n : total - 1, :]


def gather_kernel(extent, head, nsplit, planes, table, out, mat, rows, freq):
    hb = head // LANES
    qh = head // extent
    nb = out.shape[-1] // LANES
    q = planes.shape[1]
    rest = q - qh
    count = extent // (planes.shape[0] // nsplit)
    seg = lax.rem(lane_ids(rest), HALF) // SEG
    seg_tail = lax.rem(lane_ids(qh - rest), HALF) // SEG

    def unpack(j, carry):
        for m in range(count):
            acc = jnp.zeros((rest, LANES), f32)
            tail = jnp.zeros((qh - rest, LANES), f32)
            for c in range(nsplit):
                for h in range(2):
                    s = 2 * h + c
                    shift = ((s - m) * SEG) % LANES
                    lo = h * qh
                    acc = jnp.where(seg == s, pltpu.roll(planes[j * nsplit + c, lo : lo + rest, :], shift, 1), acc)
                    if h == 0:
                        tail = jnp.where(
                            seg_tail == s, pltpu.roll(planes[j * nsplit + c, rest:qh, :], shift, 1), tail
                        )
            freq[pl.ds(j * count + m, qh, stride=extent), :] = jnp.concatenate([acc, tail], axis=0)
        return carry

    lax.fori_loop(0, planes.shape[0] // nsplit, unpack, 0)

    def dft(i, carry):
        parts = [freq[pl.ds(pl.multiple_of((2 * i + e) * extent, 8), extent), :] for e in range(2)]
        for e, v in enumerate(transform(table[...], parts, -1.0)):
            rows[pl.ds(pl.multiple_of((2 * i + e) * extent, 8), extent), :] = v
        return carry

    lax.fori_loop(0, qh // 2, dft, 0, unroll=2)
    for k in range(hb):
        turned = rows[k * LANES : (k + 1) * LANES, :].T
        for a in range(8):
            first = (a % 2) * HALF + (a // 2) * 8
            out[a, :, k * LANES : (k + 1) * LANES] = turned[first : first + 8]
            if hb + k < nb:
                second = first + HALF // 2
                out[a, :, (hb + k) * LANES : (hb + k + 1) * LANES] = turned[second : second + 8]


def link_kernel(extent, links, smooth, above, below, coords, out, deficit, rot):
    nb = smooth.shape[-1] // LANES
    yb = above.shape[-1] // LANES
    lane = lane_ids()

    def rotate(values, sl):
        g = rotation_of(values)
        for i in range(3):
            for j in range(3):
                for p in range(2):
                    rot[6 * i + 2 * j + p, :, sl] = g[i][j][p]

    def rotate_own(k, carry):
        rotate([smooth[a, :, block(k)] for a in range(8)], block(k))
        return carry

    def rotate_above(k, carry):
        rotate([above[a, :, block(k)] for a in range(8)], block(nb + k))
        return carry

    lax.fori_loop(0, nb, rotate_own, 0)
    lax.fori_loop(0, yb, rotate_above, 0)
    rotate([below[a] for a in range(8)], block(nb + yb))

    def step(k, total):
        sl = block(k)
        before = block(jnp.maximum(k - 1, 0))
        after = block(k + 1)
        wrap = block(jnp.where(k == yb, 0, nb + yb))
        edge_x = coords[0, :, sl] == extent - 1
        edge_z = coords[1, :, sl] == extent - 1

        def ahead_x(e):
            cur = rot[e, :, sl]
            near = pltpu.roll(jnp.where(lane == 0, rot[e, :, after], cur), LANES - 1, 1)
            far = pltpu.roll(jnp.where(lane >= LANES - extent + 1, rot[e, :, before], cur), extent - 1, 1)
            return jnp.where(edge_x, far, near)

        def ahead_y(e):
            return rot[e, :, block(k + yb)]

        def ahead_z(e):
            cur = rot[e, :, sl]
            near = pltpu.roll(jnp.where(lane < extent, rot[e, :, after], cur), LANES - extent, 1)
            far = pltpu.roll(rot[e, :, wrap], LANES - extent, 1)
            return jnp.where(edge_z, far, near)

        for d, ahead in enumerate((ahead_x, ahead_y, ahead_z)):
            u = load_link(links, d, sl)
            own = [[(rot[6 * i + 2 * j, :, sl], rot[6 * i + 2 * j + 1, :, sl]) for j in range(3)] for i in range(3)]
            left = [
                [dot_row(own[i], [u[k2][j] for k2 in range(3)], cmul) for j in range(3)]
                for i in range(3)
            ]
            for j in range(3):
                row = [(ahead(6 * j + 2 * c), ahead(6 * j + 2 * c + 1)) for c in range(3)]
                for i in range(2):
                    v = dot_row(left[i], row, mul_conj)
                    out[d, i, j, 0, :, sl] = v[0]
                    out[d, i, j, 1, :, sl] = v[1]
                    if i == j:
                        total = total + (1.0 - v[0])
                if j == 2:
                    total = total + (1.0 - dot_row(left[2], row, mul_conj)[0])
        return total

    deficit[...] = lax.fori_loop(0, nb, step, jnp.zeros((8, LANES), f32))


def sum_kernel(n, theta, deficit, out, mine, held, send_sem, recv_sem):
    me = lax.axis_index("space")
    barrier = pltpu.get_barrier_semaphore()
    for i in range(1, n):
        pl.semaphore_signal(barrier, inc=1, device_id={"space": lax.rem(me + i, n)}, device_id_type=MESH)
    lane = lane_ids()
    t = jnp.sum(jnp.sum(theta[...], axis=1, keepdims=True), axis=0, keepdims=True)
    d = jnp.sum(deficit[...], axis=1, keepdims=True)
    mine[...] = jnp.where(lane == 0, d, jnp.where(lane == 1, t, 0.0))
    pl.semaphore_wait(barrier, n - 1)
    copies = []
    for i in range(1, n):
        copy = pltpu.make_async_remote_copy(
            src_ref=mine,
            dst_ref=held.at[i],
            send_sem=send_sem.at[i],
            recv_sem=recv_sem.at[i],
            device_id={"space": lax.rem(me + i, n)},
            device_id_type=MESH,
        )
        copy.start()
        copies.append(copy)
    for copy in copies:
        copy.wait()
    total = mine[...]
    for i in range(1, n):
        total = total + held[i]
    out[...] = total


def call(kernel, out_shape, scratch, *args, params=PARAMS):
    return pl.pallas_call(
        kernel,
        out_shape=out_shape,
        in_specs=[VM] * len(args),
        out_specs=jax.tree.map(lambda _: VM, out_shape),
        scratch_shapes=scratch,
        compiler_params=params,
    )(*args)


def dft_table(n):
    k = np.arange(n)
    angle = 2.0 * np.pi / n * ((k[:, None] * k[None, :]) % n)
    full = np.concatenate([np.cos(angle), np.sin(angle)], axis=0).astype(np.float32)
    hi = full.astype(jnp.bfloat16)
    lo = (full - hi.astype(np.float32)).astype(jnp.bfloat16)
    return np.concatenate([hi, hi, lo], axis=1)


def body(links):
    n = EXTENT
    slices, local = links.shape[0], links.shape[-1]
    devices = lax.axis_size("space")
    plane = n * n
    q = local // n
    me = lax.axis_index("space")
    odd = me % 2
    shape = lambda *s: jax.ShapeDtypeStruct(s, f32)


    table = jnp.asarray(dft_table(n))
    site = jnp.arange(local, dtype=jnp.int32)
    coords = jnp.stack([site % n, (me * q + site // n - 1) % n])
    coords = jnp.broadcast_to(coords[:, None, :], (2, slices, local))
    across = jnp.transpose(links, (1, 2, 3, 4, 0, 5))
    alg = call(algebra_kernel, shape(3, 8, slices, local), [], across)
    mid = (n // 2) * n
    y_rim = from_behind(alg[1][..., local - plane :], "space", 1)
    z_below = from_behind(alg[2][..., local - LANES :], "space", 1)
    z_above = from_behind(
        jnp.where(odd == 1, alg[2][..., mid : mid + LANES], alg[2][..., :LANES]), "space", -1
    )
    head = -(-(local // 2) // (8 * n)) * 8 * n
    qh = head // n
    nsplit = 2
    count = n * nsplit // devices
    spread, theta = call(
        functools.partial(spread_kernel, n, head, nsplit),
        (shape(devices, q, LANES), shape(slices, LANES)),
        [pltpu.VMEM((LANES, head), f32), pltpu.VMEM((head, LANES), f32), pltpu.VMEM((head, LANES), f32)],
        alg, y_rim, z_below, z_above, coords, table,
    )
    planes = lax.all_to_all(spread, "space", split_axis=0, concat_axis=0, tiled=True)
    wave_np = (4.0 * np.sin(np.pi * np.arange(n) / n) ** 2).astype(np.float32)
    wave = jnp.broadcast_to(jnp.asarray(wave_np)[:, None], (n, LANES))
    slot = (np.arange(LANES) % HALF) // SEG
    kx = (me // nsplit) * count + jnp.minimum(jnp.asarray(slot), count - 1)
    wave_lane = jnp.asarray(wave_np)[kx][None, :]
    smoothed = call(
        functools.partial(plane_kernel, n),
        shape(plane, LANES),
        [pltpu.VMEM((plane, LANES), f32), pltpu.VMEM((plane, LANES), f32)],
        planes.reshape(plane, LANES), wave, wave_lane, table,
    )
    back = lax.all_to_all(
        smoothed.reshape(devices, q, LANES), "space", split_axis=0, concat_axis=0, tiled=True
    )
    smooth = call(
        functools.partial(gather_kernel, n, head, nsplit),
        shape(8, slices, local),
        [pltpu.VMEM((LANES, head), f32), pltpu.VMEM((head, LANES), f32), pltpu.VMEM((head, LANES), f32)],
        back, table,
    )
    above = from_behind(smooth[..., :plane], "space", -1)
    below = from_behind(
        jnp.where(odd == 1, smooth[..., mid : mid + LANES], smooth[..., plane : plane + LANES]), "space", 1
    )
    turned, deficit = call(
        functools.partial(link_kernel, n),
        (shape(3, 2, 3, 2, slices, local), shape(slices, LANES)),
        [pltpu.VMEM((18, slices, local + plane + LANES), f32)],
        across, smooth, above, below, coords,
    )
    new_links = jnp.transpose(turned, (4, 0, 1, 2, 3, 5))
    sums = call(
        functools.partial(sum_kernel, devices),
        shape(slices, LANES),
        [
            pltpu.VMEM((slices, LANES), f32),
            pltpu.VMEM((devices, slices, LANES), f32),
            pltpu.SemaphoreType.DMA((devices,)),
            pltpu.SemaphoreType.DMA((devices,)),
        ],
        theta, deficit,
        params=pltpu.CompilerParams(collective_id=1, has_side_effects=True),
    )
    total = sums[0, 1]
    times = lax.axis_size("tm")
    if times > 1:
        total = lax.psum(total, "tm")
    return (new_links, total / (slices * times * n**3), sums[:, 0] / n**3)


def solution(mesh):
    placed = (P("tm", None, None, None, None, "space"),)
    return jax.shard_map(
        body,
        mesh=mesh,
        in_specs=placed,
        out_specs=(P("tm", None, None, None, None, "space"), P(), P("tm")),
        check_vma=False,
    )
```

time: 415 us -> 176 us (0.42); the launches traced: 409 us -> 176 us
  local copies, waits for them, and re-layouts: 116 us -> 19.5 us
  matrix products: 68.1 us -> 0 us
  other arithmetic: 69.1 us -> 2.24 us
  Pallas kernels: 0 us -> 59.4 us
  waiting for transfers between devices: 75.8 us -> 47.2 us
  blocking collectives: 48.7 us -> 34.3 us
  starting transfers between devices: 21.6 us -> 10.4 us
  between operations: 9.56 us -> 2.54 us
    dot_general x16 -> x0, matrix products: 68.1 us -> none  [the longest x4 26.9 us: plane_step(): with_sin = jnp.einsum(einsum_form, values, sine_table, precision=highest)]
    pallas_call x0 -> x6, Pallas kernels: none -> 59.4 us  [call(): pl.pallas_call(kernel, out_shape=out_shape, in_specs=[VM] * len(args), ou...]
    slice x77 -> x3, local copies, waits for them, and re-layouts: 52.5 us -> 2.4 us  [the longest x1 1.26 us: body(): total = sums[0, 1]]
    psum x1 -> x0, blocking collectives: 48.7 us -> none  [body(): theta_total = lax.psum(theta_part, ('tm', 'space'))]
    all_to_all x0 -> x1, blocking collectives: none -> 34.3 us  [body(): lax.all_to_all(smoothed.reshape(devices, q, LANES), 'space', split_axis=0...]
    all_to_all x2 -> x1, waiting for transfers between devices: 51.3 us -> 27.2 us  [body(): lax.all_to_all(spread, 'space', split_axis=0, concat_axis=0, tiled=True)]
    reduce_sum x11 -> x0, other arithmetic: 22.1 us -> none  [the longest x8 13 us: body(): theta_part = sum((jnp.sum(a * a) for a in algebra))]
    another operation x53 -> x1, other arithmetic: 19.2 us -> 0.03 us  [body(): coords = jnp.stack([site % n, (me * q + site // n - 1) % n])]
  transfers between devices with their start and end apart: 6 -> 6, of which waited for: 4 -> 5; matrix products, arithmetic and copies ran while one was open for 4% -> 2% of each run, Pallas kernels for 0% -> 0%
where the time goes in v1:
time: 176 us
  Pallas kernels  59.4 us (34%)
  waiting for transfers between devices  47.2 us (27%)
  blocking collectives  34.3 us (19%)
  local copies, waits for them, and re-layouts  19.5 us (11%)
  starting transfers between devices  10.4 us (6%)
  between operations  2.54 us (1%)
  other arithmetic  2.24 us (1%)
    pallas_call x6, Pallas kernels, call(): pl.pallas_call(kernel, out_shape=out_shape, in_specs=[VM] * len(args), ou...  59.4 us
    all_to_all x1, blocking collectives, body(): lax.all_to_all(smoothed.reshape(devices, q, LANES), 'space', split_axis=0...  34.3 us
    all_to_all x1, waiting for transfers between devices, body(): lax.all_to_all(spread, 'space', split_axis=0, concat_axis=0, tiled=True)  27.2 us
    ppermute x5, waiting for transfers between devices, from_behind(): lax.ppermute(block, axis, [((i - distance) % n, i) for i in range(n)])  20 us
    unnamed x18, local copies, waits for them, and re-layouts  12.3 us
    ppermute x5, starting transfers between devices, from_behind(): lax.ppermute(block, axis, [((i - distance) % n, i) for i in range(n)])  7.71 us
  transfers between devices with their start and end apart: 6, of which 5 were waited for; matrix products, arithmetic and copies ran while one was open for 2% of the time, Pallas kernels for 0%

profile of v1, /device:TPU:0, one launch (start us, length us, event | category | flops | bytes accessed | tf_op | source)
XLA Modules:
  0.0 175.6 jit_solution(14386221585260926115)
XLA Ops:
  0.6 4.3 %copy.12 = f32[8,3,2,3,2,3456]{5,0,4,3,2,1:T(8,128)} copy(f32[8,3,2,3,2,3456]{5,4,3,2,1,0:T(2,128)} %param.4) | data formatting | bytes 7962624 | tf_op args[0]
  5.0 4.4 %shard_map.67.alg = f32[3,8,8,3456]{3,2,1,0:T(8,128)} custom-call(f32[3,2,3,2,8,3456]{5,4,3,2,1,0:T(8,128)} %bitcast.12), custom_call_target="tpu_custom_call" | custom-call | tf_op jit(solution)/shard_map/pallas_call | solution.py:426
  9.4 1.5 slice_bitcast_fusion
  11.0 6.5 %collective-permute-start.2 = (f32[8,8,128]{2,1,0:T(8,128)S(1)}, f32[8,8,128]{2,1,0:T(8,128)S(1)}, u32[]{:S(2)}, u32[]{:S(2)}) collective-permute-start(f32[8,8,128]{2,1,0:T(8,128)S(1)} %get-tuple-element.19), channel_id=1, source_target_pairs={{1,0},{2,1},{3,2},{4,3},{5,4},{6,5},{7,6},{8,7},{9,8},{10,9},{11,1... | collective-permute-start | bytes 98312 | tf_op jit(solution)/shard_map/ppermute | solution.py:30
  17.4 0.0 collective-permute-start.1
  17.5 0.1 collective-permute-start
  17.5 0.1 and_select_fusion
  17.7 1.3 collective-permute-done.2.z_above
  19.0 0.0 copy-start.4
  19.0 5.3 %collective-permute-done.1.z_below = f32[8,8,128]{2,1,0:T(8,128)S(1)} collective-permute-done((f32[8,8,128]{2,1,0:T(8,128)S(1)}, f32[8,8,128]{2,1,0:T(8,128)S(1)}, u32[]{:S(2)}, u32[]{:S(2)}) %collective-permute-start.1) | collective-permute-done | bytes 32800 | tf_op jit(solution)/shard_map/ppermute | solution.py:30
  24.4 0.0 copy-start.5
  24.4 6.3 %collective-permute-done.y_rim = f32[8,8,2304]{2,1,0:T(8,128)S(1)} collective-permute-done((f32[8,8,2304]{2,1,0:T(8,128)S(1)}, f32[8,8,2304]{2,1,0:T(8,128)S(1)}, u32[]{:S(2)}, u32[]{:S(2)}) %collective-permute-start) | collective-permute-done | bytes 589856 | tf_op jit(solution)/shard_map/ppermute | solution.py:30
  30.7 0.0 copy-start.2
  30.7 0.8 broadcast_in_dim.8.coords
  31.4 0.0 copy-done.4
  31.4 0.0 copy-done.5
  31.4 0.2 copy-done.2
  31.6 0.0 copy-start.7
  31.6 0.0 copy-start
  31.6 10.9 %shard_map.68 = (f32[32,72,128]{2,1,0:T(8,128)}, f32[8,128]{1,0:T(8,128)}) custom-call(f32[3,8,8,3456]{3,2,1,0:T(8,128)} %shard_map.67.alg, f32[8,8,2304]{2,1,0:T(8,128)} %copy-done.2, f32[8,8,128]{2,1,0:T(8,128)} %copy-done.5, f32[8,8,128]{2,1,0:T(8,128)} %copy-done.4, s32[2,8,3456]{2,1,0:T(8,128)} %broadcast_in_dim.8.coords, ...), custom_call_target="tpu_custom_call" | custom-call | tf_op jit(solution)/shard_map/pallas_call | solution.py:426
  42.5 2.7 %all-to-all-start = ((f32[32,72,128]{2,1,0:T(8,128)}), f32[32,72,128]{2,1,0:T(8,128)S(1)}, u32[]{:S(2)}, u32[]{:S(2)}) async-start(f32[32,72,128]{2,1,0:T(8,128)} %get-tuple-element.7), calls=%async_computation | async-start | bytes 2359296 | tf_op jit(solution)/shard_map/all_to_all | solution.py:478
  45.2 0.0 copy-done.7
  45.2 0.0 copy-done
  45.2 1.7 gather_fusion
  46.9 27.2 %all-to-all-done = f32[32,72,128]{2,1,0:T(8,128)S(1)} async-done(((f32[32,72,128]{2,1,0:T(8,128)}), f32[32,72,128]{2,1,0:T(8,128)S(1)}, u32[]{:S(2)}, u32[]{:S(2)}) %all-to-all-start) | async-done | bytes 1179680 | tf_op jit(solution)/shard_map/all_to_all | solution.py:478
  74.2 0.0 copy-start.1
  74.2 0.8 broadcast_in_dim.9.wave
  74.9 0.2 copy-done.1
  75.2 14.7 %shard_map.69 = f32[2304,128]{1,0:T(8,128)} custom-call(f32[2304,128]{1,0:T(8,128)} %bitcast.14, f32[48,128]{1,0:T(8,128)} %broadcast_in_dim.9.wave, f32[1,128]{1,0:T(1,128)} %bitcast.17, bf16[96,144]{1,0:T(8,128)(2,1)} %constant.71.clone.table), custom_call_target="tpu_custom_call" | custom-call | tf_op jit(solution)/shard_map/pallas_call | solution.py:426
  89.9 34.3 %all_to_all.10.planes = f32[32,72,128]{2,1,0:T(8,128)} all-to-all(f32[32,72,128]{2,1,0:T(8,128)} %bitcast.15), channel_id=1, replica_groups=mesh['tm'=1,'space'=32] {'space'}, dimensions={0} | all-to-all | bytes 2359296 | tf_op jit(solution)/shard_map/all_to_all | solution.py:490
  124.2 6.9 %shard_map.70.smooth = f32[8,8,3456]{2,1,0:T(8,128)} custom-call(f32[32,72,128]{2,1,0:T(8,128)} %all_to_all.10.planes, bf16[96,144]{1,0:T(8,128)(2,1)} %constant.71.clone.table), custom_call_target="tpu_custom_call" | custom-call | tf_op jit(solution)/shard_map/pallas_call | solution.py:426
  131.1 1.1 slice.54
  132.2 1.2 collective-permute-start.3
  133.4 0.8 slice_select_fusion
  134.2 0.0 collective-permute-start.4
  134.2 7.0 %collective-permute-done.4.below = f32[8,8,128]{2,1,0:T(8,128)S(1)} collective-permute-done((f32[8,8,128]{2,1,0:T(8,128)S(1)}, f32[8,8,128]{2,1,0:T(8,128)S(1)}, u32[]{:S(2)}, u32[]{:S(2)}) %collective-permute-start.4) | collective-permute-done | bytes 32800 | tf_op jit(solution)/shard_map/ppermute | solution.py:30
  141.2 0.0 copy-start.6
  141.3 0.0 collective-permute-done.3.above
  141.3 0.6 copy-done.6
  141.9 0.0 copy-start.3
  141.9 0.8 copy-done.3
  142.7 12.1 %shard_map.71 = (f32[3,2,3,2,8,3456]{5,4,3,2,1,0:T(8,128)}, f32[8,128]{1,0:T(8,128)}) custom-call(f32[3,2,3,2,8,3456]{5,4,3,2,1,0:T(8,128)} %bitcast.13, f32[8,8,3456]{2,1,0:T(8,128)} %shard_map.70.smooth, f32[8,8,2304]{2,1,0:T(8,128)} %copy-done.3, f32[8,8,128]{2,1,0:T(8,128)} %copy-done.6, s32[2,8,3456]{2,1,0:T(8,128)} %broadcast_in_dim.8.coords), custom_call_target="tpu_custom_call" | custom-call | tf_op jit(solution)/shard_map/pallas_call | solution.py:426
  154.8 10.3 %shard_map.72 = f32[8,128]{1,0:T(8,128)} custom-call(f32[8,128]{1,0:T(8,128)} %get-tuple-element.9.theta, f32[8,128]{1,0:T(8,128)} %get-tuple-element.10.deficit), custom_call_target="tpu_custom_call" | custom-call | tf_op jit(solution)/shard_map/pallas_call | solution.py:426
  165.1 1.3 slice.44
  166.4 1.3 multiply_reduce_fusion
  167.7 6.1 %copy.10 = f32[8,3,2,3,2,3456]{5,4,3,2,1,0:T(2,128)} copy(f32[8,3,2,3,2,3456]{5,0,4,3,2,1:T(8,128)} %bitcast.16) | data formatting | bytes 7962624
  (5 shorter events, 0.1 us)
Async XLA Ops:
  11.0 8.1 %collective-permute-start.2 = (f32[8,8,128]{2,1,0:T(8,128)S(1)}, f32[8,8,128]{2,1,0:T(8,128)S(1)}, u32[]{:S(2)}, u32[]{:S(2)}) collective-permute-start(f32[8,8,128]{2,1,0:T(8,128)S(1)} %get-tuple-element.19), channel_id=1, source_target_pairs={{1,0},{2,1},{3,2},{4,3},{5,4},{6,5},{7,6},{8,7},{9,8},{10,9},{11,1... | collective-permute-start | bytes 98312 | tf_op jit(solution)/shard_map/ppermute | solution.py:30
  17.4 6.9 %collective-permute-start.1 = (f32[8,8,128]{2,1,0:T(8,128)S(1)}, f32[8,8,128]{2,1,0:T(8,128)S(1)}, u32[]{:S(2)}, u32[]{:S(2)}) collective-permute-start(f32[8,8,128]{2,1,0:T(8,128)S(1)} %get-tuple-element.20), channel_id=1, source_target_pairs={{31,0},{0,1},{1,2},{2,3},{3,4},{4,5},{5,6},{6,7},{7,8},{8,9},{9,10... | collective-permute-start | bytes 98312 | tf_op jit(solution)/shard_map/ppermute | solution.py:30
  17.5 13.2 %collective-permute-start = (f32[8,8,2304]{2,1,0:T(8,128)S(1)}, f32[8,8,2304]{2,1,0:T(8,128)S(1)}, u32[]{:S(2)}, u32[]{:S(2)}) collective-permute-start(f32[8,8,2304]{2,1,0:T(8,128)S(1)} %slice.49), channel_id=1, source_target_pairs={{31,0},{0,1},{1,2},{2,3},{3,4},{4,5},{5,6},{6,7},{7,8},{8,9},{9,10... | collective-permute-start | bytes 1769480 | tf_op jit(solution)/shard_map/ppermute | solution.py:30
  19.0 12.4 %copy-start.4 = (f32[8,8,128]{2,1,0:T(8,128)}, f32[8,8,128]{2,1,0:T(8,128)S(1)}, u32[]{:S(2)}) copy-start(f32[8,8,128]{2,1,0:T(8,128)S(1)} %collective-permute-done.2.z_above) | copy-start | bytes 98308
  24.4 7.1 %copy-start.5 = (f32[8,8,128]{2,1,0:T(8,128)}, f32[8,8,128]{2,1,0:T(8,128)S(1)}, u32[]{:S(2)}) copy-start(f32[8,8,128]{2,1,0:T(8,128)S(1)} %collective-permute-done.1.z_below) | copy-start | bytes 98308
  30.7 0.9 copy-start.2
  31.6 13.6 %copy-start.7 = (s32[128]{0:T(128)S(1)}, s32[128]{0:T(128)}, u32[]{:S(2)}) copy-start(s32[128]{0:T(128)} %constant.74) | copy-start | bytes 1540
  31.6 13.6 %copy-start = (f32[48]{0:T(128)S(1)}, f32[48]{0:T(128)}, u32[]{:S(2)}) copy-start(f32[48]{0:T(128)} %constant.72.clone) | copy-start | bytes 580
  42.5 31.7 %all-to-all-start = ((f32[32,72,128]{2,1,0:T(8,128)}), f32[32,72,128]{2,1,0:T(8,128)S(1)}, u32[]{:S(2)}, u32[]{:S(2)}) async-start(f32[32,72,128]{2,1,0:T(8,128)} %get-tuple-element.7), calls=%async_computation | async-start | bytes 2359296 | tf_op jit(solution)/shard_map/all_to_all | solution.py:478
  74.2 1.0 copy-start.1
  132.2 9.0 %collective-permute-start.3 = (f32[8,8,2304]{2,1,0:T(8,128)S(1)}, f32[8,8,2304]{2,1,0:T(8,128)S(1)}, u32[]{:S(2)}, u32[]{:S(2)}) collective-permute-start(f32[8,8,2304]{2,1,0:T(8,128)S(1)} %slice.54), channel_id=1, source_target_pairs={{1,0},{2,1},{3,2},{4,3},{5,4},{6,5},{7,6},{8,7},{9,8},{10,9},{11,1... | collective-permute-start | bytes 1769480 | tf_op jit(solution)/shard_map/ppermute | solution.py:30
  134.2 7.0 %collective-permute-start.4 = (f32[8,8,128]{2,1,0:T(8,128)S(1)}, f32[8,8,128]{2,1,0:T(8,128)S(1)}, u32[]{:S(2)}, u32[]{:S(2)}) collective-permute-start(f32[8,8,128]{2,1,0:T(8,128)S(1)} %slice_select_fusion), channel_id=1, source_target_pairs={{31,0},{0,1},{1,2},{2,3},{3,4},{4,5},{5,6},{6,7},{7,8},{8,9},{9,10... | collective-permute-start | bytes 98312 | tf_op jit(solution)/shard_map/ppermute | solution.py:30
  141.2 0.6 copy-start.6
  141.9 0.8 copy-start.3

commit v2 on v1

--- a/solution.py
+++ b/solution.py
@@ -23,11 +23,6 @@
 MESH = pl.DeviceIdType.MESH
 VM = pl.BlockSpec(memory_space=pltpu.VMEM)
 PARAMS = pltpu.CompilerParams(vmem_limit_bytes=60 * 1024 * 1024)
-
-
-def from_behind(block, axis, distance):
-    n = lax.axis_size(axis)
-    return lax.ppermute(block, axis, [((i - distance) % n, i) for i in range(n)])
 
 
 def cmul(p, q):
@@ -165,7 +160,40 @@
     return outs
 
 
-def spread_kernel(extent, head, nsplit, alg, y_rim, z_below, z_above, coords, table, out, theta, mat, rows, freq):
+def packed_rows(q, count):
+    free = HALF // SEG - count
+    moved = -(-q * free // (count + free)) // 8 * 8
+    return q - moved if free == 1 else q
+
+
+def pack_rows(full, count):
+    q = full.shape[0]
+    kept = packed_rows(q, count)
+    step = q - kept
+    if step == 0:
+        return full
+    seg = lax.rem(lane_ids(step), HALF) // SEG
+    pieces = []
+    for m in range(count):
+        moved = pltpu.roll(full[kept:], (count - m) * SEG, 1)
+        pieces.append(jnp.where(seg == count, moved, full[m * step : (m + 1) * step]))
+    return jnp.concatenate(pieces + [full[count * step : kept]], axis=0)
+
+
+def unpack_rows(block_in, q, count):
+    kept = block_in.shape[0]
+    step = q - kept
+    if step == 0:
+        return block_in
+    seg = lax.rem(lane_ids(step), HALF) // SEG
+    tail = jnp.zeros((step, LANES), f32)
+    for m in range(count):
+        moved = pltpu.roll(block_in[m * step : (m + 1) * step], LANES - (count - m) * SEG, 1)
+        tail = jnp.where(seg == m, moved, tail)
+    return jnp.concatenate([block_in, tail], axis=0)
+
+
+def spread_kernel(extent, head, nsplit, q, alg, y_rim, z_below, z_above, coords, table, out, theta, mat, rows, freq):
     nb = alg.shape[-1] // LANES
     yb = y_rim.shape[-1] // LANES
     qh = head // extent
@@ -212,32 +240,45 @@
 
     lax.fori_loop(0, qh // 2, dft, 0, unroll=2)
     count = extent // (out.shape[0] // nsplit)
-    q = out.shape[1]
     seg = lax.rem(lane_ids(qh), HALF) // SEG
 
     def pack(j, carry):
         vals = [freq[pl.ds(j * count + m, qh, stride=extent), :] for m in range(count)]
         for c in range(nsplit):
+            full = []
             for h in range(2):
                 acc = jnp.zeros((qh, LANES), f32)
                 for m in range(count):
                     moved = pltpu.roll(vals[m], ((m - (2 * h + c)) * SEG) % LANES, 1)
                     acc = jnp.where(seg == m, moved, acc)
-                lo, hi = (0, qh) if h == 0 else (qh, q)
-                out[j * nsplit + c, lo:hi, :] = acc[: hi - lo]
+                full.append(acc[: qh if h == 0 else q - qh])
+            out[j * nsplit + c] = pack_rows(jnp.concatenate(full, axis=0), count)
         return carry
 
     lax.fori_loop(0, out.shape[0] // nsplit, pack, 0)
 
 
-def plane_kernel(extent, planes, wave, wave_lane, table, out, one, two):
+def plane_kernel(extent, nsplit, planes, wave, table, out, one, two):
     n = extent
     total = n * n
+    devices, kept = planes.shape[0], planes.shape[1]
+    q = total // devices
+    count = n * nsplit // devices
     scale = top_momentum / float(n) ** 3
+
+    def fill(s, carry):
+        two[pl.ds(pl.multiple_of(s * q, 8), q), :] = unpack_rows(planes[s], q, count)
+        return carry
+
+    lax.fori_loop(0, devices, fill, 0)
     for y in range(n - 1):
-        one[y * n : (y + 1) * n, :] = planes[y * n + 1 : (y + 1) * n + 1, :]
-    one[total - n : total - 1, :] = planes[total - n + 1 : total, :]
-    one[total - 1 : total, :] = planes[0:1, :]
+        one[y * n : (y + 1) * n, :] = two[y * n + 1 : (y + 1) * n + 1, :]
+    one[total - n : total - 1, :] = two[total - n + 1 : total, :]
+    one[total - 1 : total, :] = two[0:1, :]
+    slot = jnp.minimum(lax.rem(lane_ids(n), HALF) // SEG, count - 1)
+    kx = lax.div(lax.axis_index("space"), nsplit) * count + slot
+    chosen = lax.broadcasted_iota(jnp.int32, (n, LANES), 0) == kx
+    wave_lane = jnp.sum(jnp.where(chosen, wave[...], 0.0), axis=0, keepdims=True)
 
     def rows_at(i):
         return pl.ds(pl.multiple_of(i * n, 8), n)
@@ -255,7 +296,7 @@
         vals = transform(table[...], parts, 1.0)
         done = []
         for e, v in enumerate(vals):
-            p2 = wave[...] + (wave_lane[...] + wave[pl.ds(2 * i + e, 1), :])
+            p2 = wave[...] + (wave_lane + wave[pl.ds(2 * i + e, 1), :])
             zero = p2 == 0.0
             done.append(v * jnp.where(zero, 0.0, scale / jnp.where(zero, 1.0, p2)))
         for e, v in enumerate(transform(table[...], done, -1.0)):
@@ -271,23 +312,30 @@
         return carry
 
     lax.fori_loop(0, n // 2, back_z, 0, unroll=2)
-    out[0:1, :] = two[total - 1 : total, :]
+    one[0:1, :] = two[total - 1 : total, :]
     for y in range(n - 1):
-        out[y * n + 1 : (y + 1) * n + 1, :] = two[y * n : (y + 1) * n, :]
-    out[total - n + 1 : total, :] = two[total - n : total - 1, :]
-
-
-def gather_kernel(extent, head, nsplit, planes, table, out, mat, rows, freq):
+        one[y * n + 1 : (y + 1) * n + 1, :] = two[y * n : (y + 1) * n, :]
+    one[total - n + 1 : total, :] = two[total - n : total - 1, :]
+
+    def put(s, carry):
+        out[s] = pack_rows(one[pl.ds(pl.multiple_of(s * q, 8), q), :], count)
+        return carry
+
+    lax.fori_loop(0, devices, put, 0)
+
+
+def gather_kernel(extent, head, nsplit, planes, table, out, rows, freq):
     hb = head // LANES
     qh = head // extent
     nb = out.shape[-1] // LANES
-    q = planes.shape[1]
+    q = out.shape[-1] // extent
     rest = q - qh
     count = extent // (planes.shape[0] // nsplit)
     seg = lax.rem(lane_ids(rest), HALF) // SEG
     seg_tail = lax.rem(lane_ids(qh - rest), HALF) // SEG
 
     def unpack(j, carry):
+        full = [unpack_rows(planes[j * nsplit + c], q, count) for c in range(nsplit)]
         for m in range(count):
             acc = jnp.zeros((rest, LANES), f32)
             tail = jnp.zeros((qh - rest, LANES), f32)
@@ -296,10 +344,10 @@
                     s = 2 * h + c
                     shift = ((s - m) * SEG) % LANES
                     lo = h * qh
-                    acc = jnp.where(seg == s, pltpu.roll(planes[j * nsplit + c, lo : lo + rest, :], shift, 1), acc)
+                    acc = jnp.where(seg == s, pltpu.roll(full[c][lo : lo + rest], shift, 1), acc)
                     if h == 0:
                         tail = jnp.where(
-                            seg_tail == s, pltpu.roll(planes[j * nsplit + c, rest:qh, :], shift, 1), tail
+                            seg_tail == s, pltpu.roll(full[c][rest:qh], shift, 1), tail
                         )
             freq[pl.ds(j * count + m, qh, stride=extent), :] = jnp.concatenate([acc, tail], axis=0)
         return carry
@@ -392,15 +440,88 @@
     deficit[...] = lax.fori_loop(0, nb, step, jnp.zeros((8, LANES), f32))
 
 
-def sum_kernel(n, theta, deficit, out, mine, held, send_sem, recv_sem):
+def greet(others):
+    barrier = pltpu.get_barrier_semaphore()
+    for other in others:
+        pl.semaphore_signal(barrier, inc=1, device_id={"space": other}, device_id_type=MESH)
+    return barrier
+
+
+def exchange_kernel(n, blocks, out, send_sem, recv_sem):
     me = lax.axis_index("space")
-    barrier = pltpu.get_barrier_semaphore()
+    barrier = greet([lax.rem(me + i, n) for i in range(1, n)])
+    out[me] = blocks[me]
+    pl.semaphore_wait(barrier, n - 1)
+    copies = []
     for i in range(1, n):
-        pl.semaphore_signal(barrier, inc=1, device_id={"space": lax.rem(me + i, n)}, device_id_type=MESH)
-    lane = lane_ids()
+        other = lax.rem(me + i, n)
+        copy = pltpu.make_async_remote_copy(
+            src_ref=blocks.at[other],
+            dst_ref=out.at[me],
+            send_sem=send_sem.at[i],
+            recv_sem=recv_sem.at[i],
+            device_id={"space": other},
+            device_id_type=MESH,
+        )
+        copy.start()
+        copies.append(copy)
+    for copy in copies:
+        copy.wait()
+
+
+def exchange(blocks, n, number):
+    return call(
+        functools.partial(exchange_kernel, n),
+        jax.ShapeDtypeStruct(blocks.shape, f32),
+        [pltpu.SemaphoreType.DMA((n,)), pltpu.SemaphoreType.DMA((n,))],
+        blocks,
+        params=pltpu.CompilerParams(collective_id=number, has_side_effects=True),
+    )
+
+
+def halo_kernel(n, moves, source, *refs):
+    outs, (send_sem, recv_sem) = refs[:-2], refs[-2:]
+    me = lax.axis_index("space")
+    ahead, behind = lax.rem(me + 1, n), lax.rem(me + n - 1, n)
+    barrier = greet([ahead, behind])
+    pl.semaphore_wait(barrier, 2)
+    odd = lax.rem(me, 2)
+    copies = []
+    for i, (direction, select) in enumerate(moves):
+        copy = pltpu.make_async_remote_copy(
+            src_ref=select(source, odd),
+            dst_ref=outs[i],
+            send_sem=send_sem.at[i],
+            recv_sem=recv_sem.at[i],
+            device_id={"space": ahead if direction > 0 else behind},
+            device_id_type=MESH,
+        )
+        copy.start()
+        copies.append(copy)
+    for copy in copies:
+        copy.wait()
+
+
+def halos(source, n, moves, shapes, number):
+    count = len(moves)
+    return call(
+        functools.partial(halo_kernel, n, moves),
+        shapes,
+        [pltpu.SemaphoreType.DMA((count,)), pltpu.SemaphoreType.DMA((count,))],
+        source,
+        params=pltpu.CompilerParams(collective_id=number, has_side_effects=True),
+    )
+
+
+def sum_kernel(n, scales, theta, deficit, out_theta, out_deficit, mine, held, send_sem, recv_sem):
+    me = lax.axis_index("space")
+    barrier = greet([lax.rem(me + i, n) for i in range(1, n)])
+    slices = deficit.shape[0]
+    lane = lane_ids(slices)
     t = jnp.sum(jnp.sum(theta[...], axis=1, keepdims=True), axis=0, keepdims=True)
     d = jnp.sum(deficit[...], axis=1, keepdims=True)
-    mine[...] = jnp.where(lane == 0, d, jnp.where(lane == 1, t, 0.0))
+    own = lax.broadcasted_iota(jnp.int32, (slices, LANES), 0)
+    mine[...] = jnp.where(lane == own, d, jnp.where(lane == slices, jnp.where(own == 0, t, 0.0), 0.0))
     pl.semaphore_wait(barrier, n - 1)
     copies = []
     for i in range(1, n):
@@ -419,7 +540,9 @@
     total = mine[...]
     for i in range(1, n):
         total = total + held[i]
-    out[...] = total
+    row = jnp.sum(total, axis=0, keepdims=True)
+    out_deficit[...] = row[:, :slices] * scales[1]
+    out_theta[...] = row[:, slices : slices + 1] * scales[0]
 
 
 def call(kernel, out_shape, scratch, *args, params=PARAMS):
@@ -449,7 +572,6 @@
     plane = n * n
     q = local // n
     me = lax.axis_index("space")
-    odd = me % 2
     shape = lambda *s: jax.ShapeDtypeStruct(s, f32)
 
 
@@ -460,45 +582,53 @@
     across = jnp.transpose(links, (1, 2, 3, 4, 0, 5))
     alg = call(algebra_kernel, shape(3, 8, slices, local), [], across)
     mid = (n // 2) * n
-    y_rim = from_behind(alg[1][..., local - plane :], "space", 1)
-    z_below = from_behind(alg[2][..., local - LANES :], "space", 1)
-    z_above = from_behind(
-        jnp.where(odd == 1, alg[2][..., mid : mid + LANES], alg[2][..., :LANES]), "space", -1
+    side = lambda start: pl.ds(pl.multiple_of(start, LANES), LANES)
+    y_rim, z_below, z_above = halos(
+        alg,
+        devices,
+        [
+            (1, lambda r, odd: r.at[1, :, :, local - plane :]),
+            (1, lambda r, odd: r.at[2, :, :, local - LANES :]),
+            (-1, lambda r, odd: r.at[2, :, :, side(odd * mid)]),
+        ],
+        (shape(8, slices, plane), shape(8, slices, LANES), shape(8, slices, LANES)),
+        2,
     )
     head = -(-(local // 2) // (8 * n)) * 8 * n
     qh = head // n
     nsplit = 2
-    count = n * nsplit // devices
+    kept = packed_rows(q, n * nsplit // devices)
     spread, theta = call(
-        functools.partial(spread_kernel, n, head, nsplit),
-        (shape(devices, q, LANES), shape(slices, LANES)),
+        functools.partial(spread_kernel, n, head, nsplit, q),
+        (shape(devices, kept, LANES), shape(slices, LANES)),
         [pltpu.VMEM((LANES, head), f32), pltpu.VMEM((head, LANES), f32), pltpu.VMEM((head, LANES), f32)],
         alg, y_rim, z_below, z_above, coords, table,
     )
-    planes = lax.all_to_all(spread, "space", split_axis=0, concat_axis=0, tiled=True)
+    planes = exchange(spread, devices, 3)
     wave_np = (4.0 * np.sin(np.pi * np.arange(n) / n) ** 2).astype(np.float32)
-    wave = jnp.broadcast_to(jnp.asarray(wave_np)[:, None], (n, LANES))
-    slot = (np.arange(LANES) % HALF) // SEG
-    kx = (me // nsplit) * count + jnp.minimum(jnp.asarray(slot), count - 1)
-    wave_lane = jnp.asarray(wave_np)[kx][None, :]
+    wave = jnp.asarray(np.ascontiguousarray(np.broadcast_to(wave_np[:, None], (n, LANES))))
     smoothed = call(
-        functools.partial(plane_kernel, n),
-        shape(plane, LANES),
+        functools.partial(plane_kernel, n, nsplit),
+        shape(devices, kept, LANES),
         [pltpu.VMEM((plane, LANES), f32), pltpu.VMEM((plane, LANES), f32)],
-        planes.reshape(plane, LANES), wave, wave_lane, table,
-    )
-    back = lax.all_to_all(
-        smoothed.reshape(devices, q, LANES), "space", split_axis=0, concat_axis=0, tiled=True
-    )
+        planes, wave, table,
+    )
+    back = exchange(smoothed, devices, 4)
     smooth = call(
         functools.partial(gather_kernel, n, head, nsplit),
         shape(8, slices, local),
-        [pltpu.VMEM((LANES, head), f32), pltpu.VMEM((head, LANES), f32), pltpu.VMEM((head, LANES), f32)],
+        [pltpu.VMEM((head, LANES), f32), pltpu.VMEM((head, LANES), f32)],
         back, table,
     )
-    above = from_behind(smooth[..., :plane], "space", -1)
-    below = from_behind(
-        jnp.where(odd == 1, smooth[..., mid : mid + LANES], smooth[..., plane : plane + LANES]), "space", 1
+    above, below = halos(
+        smooth,
+        devices,
+        [
+            (-1, lambda r, odd: r.at[:, :, :plane]),
+            (1, lambda r, odd: r.at[:, :, side(plane - odd * (plane - mid))]),
+        ],
+        (shape(8, slices, plane), shape(8, slices, LANES)),
+        5,
     )
     turned, deficit = call(
         functools.partial(link_kernel, n),
@@ -507,9 +637,11 @@
         across, smooth, above, below, coords,
     )
     new_links = jnp.transpose(turned, (4, 0, 1, 2, 3, 5))
-    sums = call(
-        functools.partial(sum_kernel, devices),
-        shape(slices, LANES),
+    times = lax.axis_size("tm")
+    scales = (1.0 / (slices * times * n**3), 1.0 / n**3)
+    total, shares = call(
+        functools.partial(sum_kernel, devices, scales),
+        (shape(1, 1), shape(1, slices)),
         [
             pltpu.VMEM((slices, LANES), f32),
             pltpu.VMEM((devices, slices, LANES), f32),
@@ -519,11 +651,10 @@
         theta, deficit,
         params=pltpu.CompilerParams(collective_id=1, has_side_effects=True),
     )
-    total = sums[0, 1]
-    times = lax.axis_size("tm")
+    total = total.reshape(())
     if times > 1:
         total = lax.psum(total, "tm")
-    return (new_links, total / (slices * times * n**3), sums[:, 0] / n**3)
+    return (new_links, total, shares.reshape(slices))
 
 
 def solution(mesh):

time: 176 us -> 165 us (0.938)
  Pallas kernels: 59.4 us -> 150 us
  waiting for transfers between devices: 47.2 us -> 0 us
  blocking collectives: 34.3 us -> 0 us
  starting transfers between devices: 10.4 us -> 0 us
  local copies, waits for them, and re-layouts: 19.5 us -> 11.7 us
  other arithmetic: 2.24 us -> 0.14 us
    pallas_call x6 -> x10, Pallas kernels: 59.4 us -> 150 us  [call(): pl.pallas_call(kernel, out_shape=out_shape, in_specs=[VM] * len(args), ou...]
    all_to_all x1 -> x0, blocking collectives: 34.3 us -> none  [body(): lax.all_to_all(smoothed.reshape(devices, q, LANES), 'space', split_axis=0...]
    all_to_all x1 -> x0, waiting for transfers between devices: 27.2 us -> none  [body(): lax.all_to_all(spread, 'space', split_axis=0, concat_axis=0, tiled=True)]
    ppermute x5 -> x0, waiting for transfers between devices: 20 us -> none  [from_behind(): lax.ppermute(block, axis, [((i - distance) % n, i) for i in range(n)])]
    ppermute x5 -> x0, starting transfers between devices: 7.71 us -> none  [from_behind(): lax.ppermute(block, axis, [((i - distance) % n, i) for i in range(n)])]
    all_to_all x1 -> x0, starting transfers between devices: 2.66 us -> none  [body(): lax.all_to_all(spread, 'space', split_axis=0, concat_axis=0, tiled=True)]
    slice x3 -> x0, local copies, waits for them, and re-layouts: 2.4 us -> none  [the longest x1 1.26 us: body(): total = sums[0, 1]]
    unnamed x18 -> x5, local copies, waits for them, and re-layouts: 12.3 us -> 11 us
  transfers between devices with their start and end apart: 6 -> 0, of which waited for: 5 -> 0; matrix products, arithmetic and copies ran while one was open for 2% -> 0% of each run, Pallas kernels for 0% -> 0%
where the time goes in v2:
time: 165 us; the launch traced here: 164 us
  Pallas kernels  150 us (91%)
  local copies, waits for them, and re-layouts  11.7 us (7%)
  between operations  2.39 us (1%)
    pallas_call x10, Pallas kernels, call(): pl.pallas_call(kernel, out_shape=out_shape, in_specs=[VM] * len(args), ou...  150 us
    unnamed x5, local copies, waits for them, and re-layouts  11 us

profile of v2, /device:TPU:0, one launch (start us, length us, event | category | flops | bytes accessed | tf_op | source)
XLA Modules:
  0.0 164.1 jit_solution(770566478091621937)
XLA Ops:
  0.6 0.1 and_select_fusion
  0.8 0.7 broadcast_in_dim.2.coords
  1.5 4.3 %copy.9 = f32[8,3,2,3,2,3456]{5,0,4,3,2,1:T(8,128)} copy(f32[8,3,2,3,2,3456]{5,4,3,2,1,0:T(2,128)} %param.3) | data formatting | bytes 7962624 | tf_op args[0]
  5.8 4.4 %shard_map.58.source.alg = f32[3,8,8,3456]{3,2,1,0:T(8,128)} custom-call(f32[3,2,3,2,8,3456]{5,4,3,2,1,0:T(8,128)} %bitcast.6), custom_call_target="tpu_custom_call" | custom-call | tf_op jit(solution)/shard_map/pallas_call | solution.py:549
  10.3 17.6 %shard_map.59 = (f32[8,8,2304]{2,1,0:T(8,128)}, f32[8,8,128]{2,1,0:T(8,128)}, f32[8,8,128]{2,1,0:T(8,128)}) custom-call(f32[3,8,8,3456]{3,2,1,0:T(8,128)} %shard_map.58.source.alg), custom_call_target="tpu_custom_call" | custom-call | tf_op jit(solution)/shard_map/pallas_call | solution.py:549
  27.9 11.4 %shard_map.60 = (f32[32,56,128]{2,1,0:T(8,128)}, f32[8,128]{1,0:T(8,128)}) custom-call(f32[3,8,8,3456]{3,2,1,0:T(8,128)} %shard_map.58.source.alg, f32[8,8,2304]{2,1,0:T(8,128)} %get-tuple-element.14.y_rim, f32[8,8,128]{2,1,0:T(8,128)} %get-tuple-element.15.z_below, f32[8,8,128]{2,1,0:T(8,128)} %get-tuple-element.16.z_above, ...), custom_call_target="tpu_custom_call" | custom-call | tf_op jit(solution)/shard_map/pallas_call | solution.py:549
  39.3 20.0 %shard_map.61.planes = f32[32,56,128]{2,1,0:T(8,128)} custom-call(f32[32,56,128]{2,1,0:T(8,128)} %get-tuple-element.17.blocks), custom_call_target="tpu_custom_call" | custom-call | tf_op jit(solution)/shard_map/pallas_call | solution.py:549
  59.3 19.3 %shard_map.62.blocks = f32[32,56,128]{2,1,0:T(8,128)} custom-call(f32[32,56,128]{2,1,0:T(8,128)} %shard_map.61.planes, f32[48,128]{1,0:T(8,128)} %constant.36.clone.wave, bf16[96,144]{1,0:T(8,128)(2,1)} %constant.35.clone.table), custom_call_target="tpu_custom_call" | custom-call | tf_op jit(solution)/shard_map/pallas_call | solution.py:549
  78.6 28.3 %shard_map.63.planes = f32[32,56,128]{2,1,0:T(8,128)} custom-call(f32[32,56,128]{2,1,0:T(8,128)} %shard_map.62.blocks), custom_call_target="tpu_custom_call" | custom-call | tf_op jit(solution)/shard_map/pallas_call | solution.py:549
  106.9 7.4 %shard_map.64.source.smooth = f32[8,8,3456]{2,1,0:T(8,128)} custom-call(f32[32,56,128]{2,1,0:T(8,128)} %shard_map.63.planes, bf16[96,144]{1,0:T(8,128)(2,1)} %constant.35.clone.table), custom_call_target="tpu_custom_call" | custom-call | tf_op jit(solution)/shard_map/pallas_call | solution.py:549
  114.3 19.1 %shard_map.65 = (f32[8,8,2304]{2,1,0:T(8,128)}, f32[8,8,128]{2,1,0:T(8,128)}) custom-call(f32[8,8,3456]{2,1,0:T(8,128)} %shard_map.64.source.smooth), custom_call_target="tpu_custom_call" | custom-call | tf_op jit(solution)/shard_map/pallas_call | solution.py:549
  133.4 12.1 %shard_map.66 = (f32[3,2,3,2,8,3456]{5,4,3,2,1,0:T(8,128)}, f32[8,128]{1,0:T(8,128)}) custom-call(f32[3,2,3,2,8,3456]{5,4,3,2,1,0:T(8,128)} %bitcast.7, f32[8,8,3456]{2,1,0:T(8,128)} %shard_map.64.source.smooth, f32[8,8,2304]{2,1,0:T(8,128)} %get-tuple-element.18.above, f32[8,8,128]{2,1,0:T(8,128)} %get-tuple-element.19.below, ...), custom_call_target="tpu_custom_call" | custom-call | tf_op jit(solution)/shard_map/pallas_call | solution.py:549
  145.5 10.2 %shard_map.67 = (f32[1,1]{1,0:T(1,128)}, f32[1,8]{1,0:T(1,128)}) custom-call(f32[8,128]{1,0:T(8,128)} %get-tuple-element.21.theta, f32[8,128]{1,0:T(8,128)} %get-tuple-element.22.deficit), custom_call_target="tpu_custom_call" | custom-call | tf_op jit(solution)/shard_map/pallas_call | solution.py:549
  155.8 0.0 copy-start
  155.8 6.1 %copy.7 = f32[8,3,2,3,2,3456]{5,4,3,2,1,0:T(2,128)} copy(f32[8,3,2,3,2,3456]{5,0,4,3,2,1:T(8,128)} %bitcast.8) | data formatting | bytes 7962624
  162.4 0.0 copy-done
  162.5 0.5 copy.13
  (1 shorter events, 0.0 us)
Async XLA Ops:
  155.8 6.7 %copy-start = (f32[1,8]{1,0:T(1,128)S(1)}, f32[1,8]{1,0:T(1,128)}, u32[]{:S(2)}) copy-start(f32[1,8]{1,0:T(1,128)} %get-tuple-element.24) | copy-start | bytes 100

commit v3 on v2

--- a/solution.py
+++ b/solution.py
@@ -238,7 +238,7 @@
             freq[pl.ds(pl.multiple_of((2 * i + e) * extent, 8), extent), :] = v
         return carry
 
-    lax.fori_loop(0, qh // 2, dft, 0, unroll=2)
+    lax.fori_loop(0, qh // 2, dft, 0, unroll=4)
     count = extent // (out.shape[0] // nsplit)
     seg = lax.rem(lane_ids(qh), HALF) // SEG
 
@@ -255,7 +255,7 @@
             out[j * nsplit + c] = pack_rows(jnp.concatenate(full, axis=0), count)
         return carry
 
-    lax.fori_loop(0, out.shape[0] // nsplit, pack, 0)
+    lax.fori_loop(0, out.shape[0] // nsplit, pack, 0, unroll=2)
 
 
 def plane_kernel(extent, nsplit, planes, wave, table, out, one, two):
@@ -266,15 +266,13 @@
     count = n * nsplit // devices
     scale = top_momentum / float(n) ** 3
 
-    def fill(s, carry):
-        two[pl.ds(pl.multiple_of(s * q, 8), q), :] = unpack_rows(planes[s], q, count)
-        return carry
-
-    lax.fori_loop(0, devices, fill, 0)
-    for y in range(n - 1):
-        one[y * n : (y + 1) * n, :] = two[y * n + 1 : (y + 1) * n + 1, :]
-    one[total - n : total - 1, :] = two[total - n + 1 : total, :]
-    one[total - 1 : total, :] = two[0:1, :]
+    for s in range(devices):
+        rows = unpack_rows(planes[s], q, count)
+        if s == 0:
+            one[0 : q - 1, :] = rows[1:]
+            one[total - 1 : total, :] = rows[:1]
+        else:
+            one[s * q - 1 : (s + 1) * q - 1, :] = rows
     slot = jnp.minimum(lax.rem(lane_ids(n), HALF) // SEG, count - 1)
     kx = lax.div(lax.axis_index("space"), nsplit) * count + slot
     chosen = lax.broadcasted_iota(jnp.int32, (n, LANES), 0) == kx
@@ -289,7 +287,7 @@
             two[rows_at(2 * i + e), :] = v
         return carry
 
-    lax.fori_loop(0, n // 2, along_z, 0, unroll=2)
+    lax.fori_loop(0, n // 2, along_z, 0, unroll=4)
 
     def along_y(i, carry):
         parts = [two[pl.ds(2 * i + e, n, stride=n), :] for e in range(2)]
@@ -303,7 +301,7 @@
             one[rows_at(2 * i + e), :] = v
         return carry
 
-    lax.fori_loop(0, n // 2, along_y, 0, unroll=2)
+    lax.fori_loop(0, n // 2, along_y, 0, unroll=4)
 
     def back_z(i, carry):
         parts = [one[pl.ds(2 * i + e, n, stride=n), :] for e in range(2)]
@@ -311,17 +309,13 @@
             two[rows_at(2 * i + e), :] = v
         return carry
 
-    lax.fori_loop(0, n // 2, back_z, 0, unroll=2)
-    one[0:1, :] = two[total - 1 : total, :]
-    for y in range(n - 1):
-        one[y * n + 1 : (y + 1) * n + 1, :] = two[y * n : (y + 1) * n, :]
-    one[total - n + 1 : total, :] = two[total - n : total - 1, :]
-
-    def put(s, carry):
-        out[s] = pack_rows(one[pl.ds(pl.multiple_of(s * q, 8), q), :], count)
-        return carry
-
-    lax.fori_loop(0, devices, put, 0)
+    lax.fori_loop(0, n // 2, back_z, 0, unroll=4)
+    for s in range(devices):
+        if s == 0:
+            rows = jnp.concatenate([two[total - 1 : total, :], two[0 : q - 1, :]], axis=0)
+        else:
+            rows = two[s * q - 1 : (s + 1) * q - 1, :]
+        out[s] = pack_rows(rows, count)
 
 
 def gather_kernel(extent, head, nsplit, planes, table, out, rows, freq):
@@ -352,7 +346,7 @@
             freq[pl.ds(j * count + m, qh, stride=extent), :] = jnp.concatenate([acc, tail], axis=0)
         return carry
 
-    lax.fori_loop(0, planes.shape[0] // nsplit, unpack, 0)
+    lax.fori_loop(0, planes.shape[0] // nsplit, unpack, 0, unroll=2)
 
     def dft(i, carry):
         parts = [freq[pl.ds(pl.multiple_of((2 * i + e) * extent, 8), extent), :] for e in range(2)]
@@ -360,7 +354,7 @@
             rows[pl.ds(pl.multiple_of((2 * i + e) * extent, 8), extent), :] = v
         return carry
 
-    lax.fori_loop(0, qh // 2, dft, 0, unroll=2)
+    lax.fori_loop(0, qh // 2, dft, 0, unroll=4)
     for k in range(hb):
         turned = rows[k * LANES : (k + 1) * LANES, :].T
         for a in range(8):
@@ -449,12 +443,22 @@
 
 def exchange_kernel(n, blocks, out, send_sem, recv_sem):
     me = lax.axis_index("space")
-    barrier = greet([lax.rem(me + i, n) for i in range(1, n)])
+
+    def partner(i):
+        if n & (n - 1):
+            return lax.rem(me + i, n)
+        other = me
+        for b in range(n.bit_length() - 1):
+            if i >> b & 1:
+                other = other + (1 << b) * (1 - 2 * lax.rem(lax.div(me, 1 << b), 2))
+        return other
+
+    barrier = greet([partner(i) for i in range(1, n)])
     out[me] = blocks[me]
     pl.semaphore_wait(barrier, n - 1)
     copies = []
-    for i in range(1, n):
-        other = lax.rem(me + i, n)
+    for i in reversed(range(1, n)):
+        other = partner(i)
         copy = pltpu.make_async_remote_copy(
             src_ref=blocks.at[other],
             dst_ref=out.at[me],

time: 165 us -> 149 us (0.903)
  Pallas kernels: 150 us -> 134 us
    pallas_call x10, Pallas kernels: 150 us -> 134 us  [call(): pl.pallas_call(kernel, out_shape=out_shape, in_specs=[VM] * len(args), ou...]
where the time goes in v3:
time: 149 us
  Pallas kernels  134 us (90%)
  local copies, waits for them, and re-layouts  11.7 us (8%)
  between operations  2.39 us (2%)
    pallas_call x10, Pallas kernels, call(): pl.pallas_call(kernel, out_shape=out_shape, in_specs=[VM] * len(args), ou...  134 us
    unnamed x5, local copies, waits for them, and re-layouts  11 us

profile of v3, /device:TPU:0, one launch (start us, length us, event | category | flops | bytes accessed | tf_op | source)
XLA Modules:
  0.0 148.5 jit_solution(11400114935894707119)
XLA Ops:
  0.6 0.1 and_select_fusion
  0.8 0.7 broadcast_in_dim.2.coords
  1.5 4.3 %copy.9 = f32[8,3,2,3,2,3456]{5,0,4,3,2,1:T(8,128)} copy(f32[8,3,2,3,2,3456]{5,4,3,2,1,0:T(2,128)} %param.3) | data formatting | bytes 7962624 | tf_op args[0]
  5.8 4.4 %shard_map.58.source.alg = f32[3,8,8,3456]{3,2,1,0:T(8,128)} custom-call(f32[3,2,3,2,8,3456]{5,4,3,2,1,0:T(8,128)} %bitcast.6), custom_call_target="tpu_custom_call" | custom-call | tf_op jit(solution)/shard_map/pallas_call | solution.py:553
  10.3 17.6 %shard_map.59 = (f32[8,8,2304]{2,1,0:T(8,128)}, f32[8,8,128]{2,1,0:T(8,128)}, f32[8,8,128]{2,1,0:T(8,128)}) custom-call(f32[3,8,8,3456]{3,2,1,0:T(8,128)} %shard_map.58.source.alg), custom_call_target="tpu_custom_call" | custom-call | tf_op jit(solution)/shard_map/pallas_call | solution.py:553
  27.9 9.6 %shard_map.60 = (f32[32,56,128]{2,1,0:T(8,128)}, f32[8,128]{1,0:T(8,128)}) custom-call(f32[3,8,8,3456]{3,2,1,0:T(8,128)} %shard_map.58.source.alg, f32[8,8,2304]{2,1,0:T(8,128)} %get-tuple-element.14.y_rim, f32[8,8,128]{2,1,0:T(8,128)} %get-tuple-element.15.z_below, f32[8,8,128]{2,1,0:T(8,128)} %get-tuple-element.16.z_above, ...), custom_call_target="tpu_custom_call" | custom-call | tf_op jit(solution)/shard_map/pallas_call | solution.py:553
  37.5 26.6 %shard_map.61.planes = f32[32,56,128]{2,1,0:T(8,128)} custom-call(f32[32,56,128]{2,1,0:T(8,128)} %get-tuple-element.17.blocks), custom_call_target="tpu_custom_call" | custom-call | tf_op jit(solution)/shard_map/pallas_call | solution.py:553
  64.1 9.6 %shard_map.62.blocks = f32[32,56,128]{2,1,0:T(8,128)} custom-call(f32[32,56,128]{2,1,0:T(8,128)} %shard_map.61.planes, f32[48,128]{1,0:T(8,128)} %constant.36.clone.wave, bf16[96,144]{1,0:T(8,128)(2,1)} %constant.35.clone.table), custom_call_target="tpu_custom_call" | custom-call | tf_op jit(solution)/shard_map/pallas_call | solution.py:553
  73.7 27.9 %shard_map.63.planes = f32[32,56,128]{2,1,0:T(8,128)} custom-call(f32[32,56,128]{2,1,0:T(8,128)} %shard_map.62.blocks), custom_call_target="tpu_custom_call" | custom-call | tf_op jit(solution)/shard_map/pallas_call | solution.py:553
  101.6 5.5 %shard_map.64.source.smooth = f32[8,8,3456]{2,1,0:T(8,128)} custom-call(f32[32,56,128]{2,1,0:T(8,128)} %shard_map.63.planes, bf16[96,144]{1,0:T(8,128)(2,1)} %constant.35.clone.table), custom_call_target="tpu_custom_call" | custom-call | tf_op jit(solution)/shard_map/pallas_call | solution.py:553
  107.1 10.8 %shard_map.65 = (f32[8,8,2304]{2,1,0:T(8,128)}, f32[8,8,128]{2,1,0:T(8,128)}) custom-call(f32[8,8,3456]{2,1,0:T(8,128)} %shard_map.64.source.smooth), custom_call_target="tpu_custom_call" | custom-call | tf_op jit(solution)/shard_map/pallas_call | solution.py:553
  117.9 12.1 %shard_map.66 = (f32[3,2,3,2,8,3456]{5,4,3,2,1,0:T(8,128)}, f32[8,128]{1,0:T(8,128)}) custom-call(f32[3,2,3,2,8,3456]{5,4,3,2,1,0:T(8,128)} %bitcast.7, f32[8,8,3456]{2,1,0:T(8,128)} %shard_map.64.source.smooth, f32[8,8,2304]{2,1,0:T(8,128)} %get-tuple-element.18.above, f32[8,8,128]{2,1,0:T(8,128)} %get-tuple-element.19.below, ...), custom_call_target="tpu_custom_call" | custom-call | tf_op jit(solution)/shard_map/pallas_call | solution.py:553
  129.9 10.2 %shard_map.67 = (f32[1,1]{1,0:T(1,128)}, f32[1,8]{1,0:T(1,128)}) custom-call(f32[8,128]{1,0:T(8,128)} %get-tuple-element.21.theta, f32[8,128]{1,0:T(8,128)} %get-tuple-element.22.deficit), custom_call_target="tpu_custom_call" | custom-call | tf_op jit(solution)/shard_map/pallas_call | solution.py:553
  140.2 0.0 copy-start
  140.2 6.1 %copy.7 = f32[8,3,2,3,2,3456]{5,4,3,2,1,0:T(2,128)} copy(f32[8,3,2,3,2,3456]{5,0,4,3,2,1:T(8,128)} %bitcast.8) | data formatting | bytes 7962624
  146.9 0.0 copy-done
  146.9 0.5 copy.13
  (1 shorter events, 0.0 us)
Async XLA Ops:
  140.2 6.7 %copy-start = (f32[1,8]{1,0:T(1,128)S(1)}, f32[1,8]{1,0:T(1,128)}, u32[]{:S(2)}) copy-start(f32[1,8]{1,0:T(1,128)} %get-tuple-element.24) | copy-start | bytes 100
